TPU v7x, 128 devices: a whole 4x4x4 slice. The times are simulated.
128 devices in a mesh: gx: 16 (over x_lo, y, core), gy: 8 (over z, x_hi).
Axes of the slice: x: 4 (x_hi: 2, x_lo: 2; x = x_hi * 2 + x_lo), y: 4, z: 4, core: 2. Of those that a mesh axis runs over, the one named last changes fastest.
Arguments:
- collocation: bfloat16 [3072, 16384], P(None, 'gx'), may hold values from -6 to 6
- density: bfloat16 [3072, 3072], P('gy'), may hold values from -0.109375 to 0.109375
- kernel: bfloat16 [16384, 16, 8, 128], P('gx', None, 'gy'), may hold values from -6.67572e-06 to 6.67572e-06
Outputs:
- exchange: float32 [3072, 3072], P('gx', 'gy')
All inputs are finite; a program needn't handle non-finite values.
Results may differ from a plain program's by a relative error of at most 0.008.
Values may be sent and summed in bfloat16 or wider, within the bound.
No kernel may reach another device: no remote copies, remote signals or barrier semaphores. Data moves between devices by JAX's collectives and lax.ppermute only.
A program may use at most 448 MiB of HBM per device.

v0:
```python
import jax
import jax.numpy as jnp
from jax import lax
from jax.sharding import PartitionSpec as P


def in_blocks(array, dim, count):
    before, after = (array.shape[:dim], array.shape[dim + 1 :])
    return jnp.moveaxis(array.reshape(*before, count, -1, *after), dim, 0)


def summed_on_arrival(array, axis, dim):
    parts = in_blocks(array, dim, lax.axis_size(axis))
    arrived = lax.all_to_all(parts, axis, split_axis=0, concat_axis=0, tiled=True)
    return arrived.astype(jnp.float32).sum(axis=0)


def local(collocation, density, kernel):
    piece_width = kernel.shape[3]
    column_group = lax.axis_index("gy")
    own_rows = jnp.dot(density, collocation, preferred_element_type=jnp.float32).astype(
        jnp.bfloat16
    )
    dense_block = lax.all_gather(own_rows, "gy", axis=0, tiled=True)
    own_piece = lax.dynamic_slice_in_dim(collocation, column_group * piece_width, piece_width, 1)
    kernel_tiles = kernel[:, :, 0, :]
    panel_rows = kernel_tiles.shape[0]
    pieces = lax.all_gather(own_piece, "gx", axis=1, tiled=True)
    panels_in = pieces.shape[1] // piece_width
    products = lax.dot_general(
        dense_block, pieces, (((0,), (0,)), ((), ())), preferred_element_type=jnp.float32
    )
    coefficients = kernel_tiles
    coefficients = coefficients.reshape(panel_rows, panels_in * piece_width)
    weighted = (coefficients.astype(jnp.float32) * products).astype(jnp.bfloat16)
    partial_value = lax.dot_general(
        weighted, pieces, (((1,), (1,)), ((), ())), preferred_element_type=jnp.float32
    )
    reduced = summed_on_arrival(partial_value.astype(jnp.bfloat16), "gy", 1).astype(jnp.bfloat16)
    return summed_on_arrival(
        jnp.dot(collocation, reduced, preferred_element_type=jnp.float32).astype(jnp.bfloat16),
        "gx",
        0,
    )


def solution(mesh):
    return jax.shard_map(
        local,
        mesh=mesh,
        in_specs=(P(None, "gx"), P("gy", None), P("gx", None, "gy", None)),
        out_specs=P("gx", "gy"),
        check_vma=False,
    )
```

profile of v0, /device:TPU:1, one launch (start us, length us, event | category | flops | bytes accessed | tf_op | source)
XLA Modules:
  0.0 359.7 jit_solution(601240822432867312)
XLA Ops:
  6.5 0.0 copy-start
  6.5 0.0 all-gather.3.cloned.1.call-start
  6.5 1.7 copy-done
  8.2 6.3 %convolution_convert_fusion.2 = bf16[384,1024]{1,0:T(8,128)(2,1)} fusion(bf16[384,3072]{1,0:T(8,128)(2,1)S(1)} %copy-done, bf16[3072,1024]{1,0:T(8,128)(2,1)} %param.3), kind=kOutput, calls=%fused_computation.7 | convolution fusion | flops 2416312320 | bytes 9437184 | tf_op jit(solution)/shard_map/dot_general | solution.py:21
  14.5 0.0 all-gather.3.cloned.1.call-update
  14.5 0.0 all-gather.5.cloned.1.call-start
  14.5 2.1 constant_dynamic-slice_fusion
  16.6 0.0 all-gather.5.cloned.1.call-update
  16.6 6.5 %convert.2 = f32[128,8,16,128]{3,2,1,0:T(8,128)} convert(bf16[128,8,16,128]{3,2,1,0:T(8,128)(2,1)} %bitcast.29) | non-fusion elementwise | flops 2097152 | bytes 12582912
  23.1 82.7 %all-gather.3.cloned.1.call-done = bf16[3072,1024]{1,0:T(8,128)(2,1)} async-done(((bf16[384,1024]{1,0:T(8,128)(2,1)}), bf16[3072,1024]{1,0:T(8,128)(2,1)}) %all-gather.3.cloned.1.call-update) | async-done | bytes 6291472 | tf_op jit(solution)/shard_map/all_gather | solution.py:24
  105.9 78.3 %all-gather.5.cloned.1.call-done = bf16[3072,2048]{1,0:T(8,128)(2,1)} async-done(((bf16[3072,128]{1,0:T(8,128)(2,1)}), bf16[3072,2048]{1,0:T(8,128)(2,1)}) %all-gather.5.cloned.1.call-update) | async-done | bytes 12582928 | tf_op jit(solution)/shard_map/all_gather | solution.py:28
  184.2 21.6 %fusion = bf16[1024,2048]{1,0:T(8,128)(2,1)S(1)} fusion(f32[128,8,16,128]{3,2,1,0:T(8,128)} %convert.2, bf16[3072,1024]{1,0:T(8,128)(2,1)} %all-gather.3.cloned.1.call-done, bf16[3072,2048]{1,0:T(8,128)(2,1)} %all-gather.5.cloned.1.call-done), kind=kOutput, calls=%fused_computation.1 | convolution fusion | flops 12889096192 | bytes 31457280 | tf_op jit(solution)/shard_map/dot_general | solution.py:30
  205.8 16.1 %convolution_convert_fusion = bf16[1024,3072]{1,0:T(8,128)(2,1)S(1)} fusion(bf16[1024,2048]{1,0:T(8,128)(2,1)S(1)} %fusion, bf16[3072,2048]{1,0:T(8,128)(2,1)} %all-gather.5.cloned.1.call-done), kind=kOutput, calls=%fused_computation.3 | convolution fusion | flops 12888047616 | bytes 23068672 | tf_op jit(solution)/shard_map/dot_general | solution.py:36
  221.9 0.7 copy.11
  222.6 78.8 %all_to_all.10 = bf16[8,1024,384]{2,1,0:T(8,128)(2,1)} all-to-all(bf16[8,1024,384]{2,1,0:T(8,128)(2,1)S(1)} %bitcast.26), channel_id=1, replica_groups=mesh['gx'=16,'gy'=8] {'gy'}, dimensions={0} | all-to-all | bytes 12582912 | tf_op jit(solution)/shard_map/all_to_all | solution.py:14
  301.4 4.1 %reduce_sum.21 = bf16[1024,384]{1,0:T(8,128)(2,1)S(1)} reduce(bf16[8,1024,384]{2,1,0:T(8,128)(2,1)} %all_to_all.10, bf16[]{:T(256)} %constant.12.clone.1), dimensions={0}, to_apply=%region_0.0 | reduce | flops 2752512 | bytes 7077890 | tf_op jit(solution)/shard_map/reduce_sum | solution.py:15
  305.6 0.0 copy-start.1
  305.6 7.0 %fusion.1 = bf16[3072,384]{0,1:T(8,128)(2,1)} fusion(bf16[1024,384]{1,0:T(8,128)(2,1)S(1)} %reduce_sum.21, bf16[3072,1024]{1,0:T(8,128)(2,1)} %param.3), kind=kOutput, calls=%fused_computation.6 | convolution fusion | flops 2417098752 | bytes 9437184 | tf_op jit(solution)/shard_map/dot_general | solution.py:41
  312.6 4.3 %copy.6 = bf16[3072,384]{1,0:T(8,128)(2,1)} copy(bf16[3072,384]{0,1:T(8,128)(2,1)} %fusion.1) | data formatting | bytes 4718592 | tf_op jit(solution)/shard_map/convert_element_type | solution.py:41
  316.9 34.9 %all_to_all.11 = bf16[16,192,384]{2,1,0:T(8,128)(2,1)S(1)} all-to-all(bf16[16,192,384]{2,1,0:T(8,128)(2,1)} %bitcast.27), channel_id=1, replica_groups=mesh['gx'=16,'gy'=8] {'gx'}, dimensions={0} | all-to-all | bytes 4718592 | tf_op jit(solution)/shard_map/all_to_all | solution.py:14
  351.8 1.0 convert_reduce_fusion
  352.8 0.0 copy-done.1
Async XLA Ops:
  6.5 1.7 copy-start
  6.5 99.3 %all-gather.3.cloned.1.call-start = ((), (), s32[]{:S(2)}) async-start(), calls=%async_computation.2 | async-start | bytes 7077888 | tf_op jit(solution)/shard_map/all_gather | solution.py:24
  14.5 169.7 %all-gather.5.cloned.1.call-start = ((), (), s32[]{:S(2)}) async-start(), calls=%async_computation.3 | async-start | bytes 13369344 | tf_op jit(solution)/shard_map/all_gather | solution.py:28
  305.6 47.3 %copy-start.1 = (bf16[384,3072]{1,0:T(8,128)(2,1)S(1)}, bf16[384,3072]{1,0:T(8,128)(2,1)}, u32[]{:S(2)}) copy-start(bf16[384,3072]{1,0:T(8,128)(2,1)} %param.4) | copy-start | bytes 7077892
Sparse Core Ops, SparseCore 0:
  14.6 91.2 all-gather.2
  107.5 76.6 all-gather.4
where the time goes:
time: 360 us
  waiting for transfers between devices  161 us (45%)
  blocking collectives  114 us (32%)
  matrix products  51 us (14%)
  between operations  13.4 us (4%)
  other arithmetic  11.6 us (3%)
  local copies, waits for them, and re-layouts  8.69 us (2%)
    all_to_all x2, blocking collectives, summed_on_arrival(): lax.all_to_all(parts, axis, split_axis=0, concat_axis=0, tiled=True)  114 us
    all_gather x1, waiting for transfers between devices, local(): dense_block = lax.all_gather(own_rows, 'gy', axis=0, tiled=True)  82.7 us
    all_gather x1, waiting for transfers between devices, local(): pieces = lax.all_gather(own_piece, 'gx', axis=1, tiled=True)  78.3 us
    dot_general x1, matrix products, local(): lax.dot_general(dense_block, pieces, (((0,), (0,)), ((), ())), preferred_...  21.6 us
    dot_general x1, matrix products, local(): lax.dot_general(weighted, pieces, (((1,), (1,)), ((), ())), preferred_ele...  16.1 us
  transfers between devices with their start and end apart: 2, of which 2 were waited for; matrix products, arithmetic and copies ran while one was open for 2% of the time, Pallas kernels for 0%

commit v1 on v0

v1 whole, which is shorter than its diff:
```python
import functools

import jax
import jax.numpy as jnp
from jax import lax
from jax.experimental import pallas as pl
from jax.experimental.pallas import tpu as pltpu
from jax.sharding import PartitionSpec as P


BF = jnp.bfloat16
F32 = jnp.float32
ANY = pl.BlockSpec(memory_space=pl.ANY)
SMEM = pl.BlockSpec(memory_space=pltpu.SMEM)
VMEM_LIMIT = 60 * 1024 * 1024
AT_Z, AT_ROWS, AT_X = 25, 28, 44


def gx_pairs(f):
    out = []
    for a in range(2):
        for b in range(4):
            for c in range(2):
                ta, tb, tc = f(a, b, c)
                out.append(((a * 4 + b) * 2 + c, (ta * 4 + tb % 4) * 2 + tc))
    return out


def gy_pairs(f):
    out = []
    for z in range(4):
        for h in range(2):
            tz, th = f(z, h)
            out.append((z * 2 + h, (tz % 4) * 2 + th))
    return out


def both_pairs(f):
    out = []
    for g in range(16):
        for z in range(4):
            for h in range(2):
                tz, th = f(g % 2, z, h)
                out.append((g * 8 + z * 2 + h, g * 8 + (tz % 4) * 2 + th))
    return out


CORE = gx_pairs(lambda a, b, c: (a, b, 1 - c))
XLO = gx_pairs(lambda a, b, c: (1 - a, b, c))
YSPLIT = gx_pairs(lambda a, b, c: (a, b + 1 if c == 0 else b - 1, c))
ZSPLIT = both_pairs(lambda c, z, h: (z + 1 if c == 0 else z - 1, h))
XHI = gy_pairs(lambda z, h: (z, 1 - h))
ZUP = gy_pairs(lambda z, h: (z + 1, h))
ZDOWN = gy_pairs(lambda z, h: (z - 1, h))


def gx_perm(x, pairs):
    return lax.ppermute(x, "gx", pairs)


def gy_perm(x, pairs):
    return lax.ppermute(x, "gy", pairs)


def both_perm(x, pairs):
    return lax.ppermute(x, ("gx", "gy"), pairs)


def after(x, *others):
    return lax.optimization_barrier((x, *others))[0]


def lanes(ref, first, n, rows=slice(None)):
    return jnp.concatenate([ref[first + i, rows, :] for i in range(n)], axis=1)


def ahead(q, n, limit, fetch):
    for k in range(n, limit):
        pl.when(q + n == k)(functools.partial(fetch, k))


def early_kernel(n_d, n_c, mu, tab, *refs):
    d_refs, c_refs, o_ref = refs[:n_d], refs[n_d : n_d + n_c], refs[n_d + n_c]
    d_s, c_s, o_s, d_sem, c_sem, o_sem = refs[n_d + n_c + 1 :]

    def c_copy(ref, p, j, rows):
        return pltpu.make_async_copy(
            ref.at[pl.ds(rows, mu), :], c_s.at[p, pl.ds(j * mu, mu), :], c_sem.at[p, j]
        )

    def o_copy(q):
        return pltpu.make_async_copy(o_s.at[q], o_ref.at[q], o_sem.at[q])

    def fetch(q):
        for p in range(4 * q, 4 * q + 4):
            for j in range(n_d):
                c_copy(c_refs[p], p, j, pl.multiple_of(tab[j] * mu, mu)).start()

    for j in range(n_d):
        pltpu.make_async_copy(d_refs[j], d_s.at[j], d_sem.at[j]).start()
    fetch(0)
    for j in range(n_d):
        pltpu.make_async_copy(d_refs[j], d_s.at[j], d_sem.at[j]).wait()
    fetch(1)

    def tile(q, carry):
        for i in range(4):
            for j in range(n_d):
                c_copy(c_refs[0], 4 * q + i, j, 0).wait()
        ahead(q, 2, n_c // 4, fetch)
        for h in range(2):
            o_s[2 * q + h] = jnp.dot(
                lanes(d_s, 0, n_d), lanes(c_s, 4 * q + 2 * h, 2), preferred_element_type=F32
            ).astype(BF)
        o_copy(2 * q).start()
        o_copy(2 * q + 1).start()
        return carry

    lax.fori_loop(0, n_c // 4, tile, 0)
    for q in range(n_c // 4):
        o_copy(2 * q).wait()
        o_copy(2 * q + 1).wait()


def early(tab, blocks, pieces, mu):
    n_d, n_c = len(blocks), len(pieces)
    panel = blocks[0].shape[0]
    return pl.pallas_call(
        functools.partial(early_kernel, n_d, n_c, mu),
        out_shape=jax.ShapeDtypeStruct((n_c // 2, panel, 256), BF),
        in_specs=[SMEM] + [ANY] * (n_d + n_c),
        out_specs=ANY,
        scratch_shapes=[
            pltpu.VMEM((n_d, panel, mu), BF),
            pltpu.VMEM((n_c, n_d * mu, 128), BF),
            pltpu.VMEM((n_c // 2, panel, 256), BF),
            pltpu.SemaphoreType.DMA((n_d,)),
            pltpu.SemaphoreType.DMA((n_c, n_d)),
            pltpu.SemaphoreType.DMA((n_c // 2,)),
        ],
        compiler_params=pltpu.CompilerParams(vmem_limit_bytes=VMEM_LIMIT),
        cost_estimate=pl.CostEstimate(
            flops=2 * panel * n_c * 128 * n_d * mu, bytes_accessed=24 << 20, transcendentals=0
        ),
        name="early",
    )(tab, *blocks, *pieces)


def weigh_kernel(n_d, n_c, mu, first, tab, *refs):
    acc_ref, z_ref = refs[:2]
    d_refs, c_refs = refs[2 : 2 + n_d], refs[2 + n_d : 2 + n_d + n_c]
    outs = refs[2 + n_d + n_c : 7 + n_d + n_c]
    w_out, u_outs = outs[0], outs[1:]
    d_s, c_s, f_s, z_s, w_s, u_s, d_sem, c_sem, f_sem, z_sem, a_sem, o_sem, u_sem = refs[
        7 + n_d + n_c :
    ]
    width = 2 * mu
    tiles = n_c // 2

    def c_copy(ref, p, j, rows):
        return pltpu.make_async_copy(
            ref.at[pl.ds(rows, mu), :], c_s.at[p, pl.ds(j * mu, mu), :], c_sem.at[p, j]
        )

    def z_copy(p, k):
        return pltpu.make_async_copy(z_ref.at[k], z_s.at[p], z_sem.at[p])

    def acc_copy(q):
        return pltpu.make_async_copy(acc_ref.at[q], w_s.at[q], a_sem.at[q])

    def far_copy(p):
        rows = pl.multiple_of(tab[24] * width, width)
        return pltpu.make_async_copy(c_refs[p].at[pl.ds(rows, width), :], f_s.at[p], f_sem.at[p])

    def w_copy(q):
        return pltpu.make_async_copy(w_s.at[q], w_out.at[q], o_sem.at[q])

    for j in range(n_d):
        pltpu.make_async_copy(d_refs[j], d_s.at[j], d_sem.at[j]).start()

    def fetch(q):
        for p in (2 * q, 2 * q + 1):
            for j in range(n_d):
                c_copy(c_refs[p], p, j, pl.multiple_of(tab[first + j] * mu, mu)).start()
            z_copy(p, tab[8 + p]).start()
        acc_copy(q).start()

    def fetch_far(q):
        for p in (2 * q, 2 * q + 1):
            far_copy(p).start()

    for q in range(2):
        fetch(q)
    for j in range(n_d):
        pltpu.make_async_copy(d_refs[j], d_s.at[j], d_sem.at[j]).wait()
    fetch(2)

    def tile(q, carry):
        for i in range(2):
            for j in range(n_d):
                c_copy(c_refs[0], 2 * q + i, j, 0).wait()
            z_copy(2 * q + i, 0).wait()
        acc_copy(q).wait()
        ahead(q, 3, tiles, fetch)
        ahead(q, 0, tiles, fetch_far)
        product = jnp.dot(
            lanes(d_s, 0, n_d), lanes(c_s, 2 * q, 2), preferred_element_type=F32
        )
        product = product + w_s[q].astype(F32)
        w_s[q] = (lanes(z_s, 2 * q, 2).astype(F32) * product).astype(BF)
        w_copy(q).start()
        return carry

    lax.fori_loop(0, tiles, tile, 0)
    for p in range(n_c):
        far_copy(p).wait()

    quarter = u_s.shape[0] // 4

    def u_copy(i):
        return pltpu.make_async_copy(
            u_s.at[pl.ds(i * quarter, quarter), :], u_outs[i], u_sem.at[i]
        )

    for i in range(4):
        part = pl.ds(i * quarter, quarter)
        u_s[part, :] = lax.dot_general(
            lanes(w_s, 0, tiles, part), lanes(f_s, 0, n_c), (((1,), (1,)), ((), ())),
            preferred_element_type=F32,
        ).astype(BF)
        u_copy(i).start()
    for q in range(tiles):
        w_copy(q).wait()
    for i in range(4):
        u_copy(i).wait()


def weigh(tab, acc, tiles, blocks, pieces, mu, first):
    n_d, n_c = len(blocks), len(pieces)
    panel = blocks[0].shape[0]
    part = jax.ShapeDtypeStruct((panel // 4, 2 * mu), BF)
    return pl.pallas_call(
        functools.partial(weigh_kernel, n_d, n_c, mu, first),
        out_shape=(jax.ShapeDtypeStruct((n_c // 2, panel, 256), BF), part, part, part, part),
        in_specs=[SMEM] + [ANY] * (n_d + n_c + 2),
        out_specs=(ANY,) * 5,
        scratch_shapes=[
            pltpu.VMEM((n_d, panel, mu), BF),
            pltpu.VMEM((n_c, n_d * mu, 128), BF),
            pltpu.VMEM((n_c, 2 * mu, 128), BF),
            pltpu.VMEM((n_c, panel, 128), BF),
            pltpu.VMEM((n_c // 2, panel, 256), BF),
            pltpu.VMEM((panel, 2 * mu), BF),
            pltpu.SemaphoreType.DMA((n_d,)),
            pltpu.SemaphoreType.DMA((n_c, n_d)),
            pltpu.SemaphoreType.DMA((n_c,)),
            pltpu.SemaphoreType.DMA((n_c,)),
            pltpu.SemaphoreType.DMA((n_c // 2,)),
            pltpu.SemaphoreType.DMA((n_c // 2,)),
            pltpu.SemaphoreType.DMA((4,)),
        ],
        compiler_params=pltpu.CompilerParams(vmem_limit_bytes=VMEM_LIMIT),
        cost_estimate=pl.CostEstimate(
            flops=2 * panel * n_c * 128 * (n_d + 2) * mu, bytes_accessed=24 << 20, transcendentals=0
        ),
        name="weigh",
    )(tab, acc, tiles, *blocks, *pieces)


def spread_kernel(n_c, mu, at, n_out, tab, *refs):
    w_ref, c_refs = refs[0], refs[1 : 1 + n_c]
    o_ref = refs[1 + n_c]
    w_s, c_s, u_s, w_sem, c_sem, o_sem = refs[2 + n_c :]
    width = 2 * mu

    def c_copy(ref, p, i, rows):
        return pltpu.make_async_copy(
            ref.at[pl.ds(rows, width), :], c_s.at[i, p], c_sem.at[i, p]
        )

    w_copy = pltpu.make_async_copy(w_ref, w_s, w_sem)
    w_copy.start()
    for i in range(n_out):
        for p in range(n_c):
            c_copy(c_refs[p], p, i, pl.multiple_of(tab[at + i] * width, width)).start()
        if i == 0:
            w_copy.wait()

    def block(i, carry):
        for p in range(n_c):
            c_copy(c_refs[0], p, i, 0).wait()
        u_s[i] = lax.dot_general(
            lanes(w_s, 0, n_c // 2), lanes(c_s.at[i], 0, n_c), (((1,), (1,)), ((), ())),
            preferred_element_type=F32,
        ).astype(BF)
        pltpu.make_async_copy(u_s.at[i], o_ref.at[i], o_sem.at[i]).start()
        return carry

    lax.fori_loop(0, n_out, block, 0)
    for i in range(n_out):
        pltpu.make_async_copy(u_s.at[i], o_ref.at[i], o_sem.at[i]).wait()


def spread(tab, weighted, pieces, mu, at, n_out):
    n_c = len(pieces)
    panel = weighted.shape[1]
    width = 2 * mu
    return pl.pallas_call(
        functools.partial(spread_kernel, n_c, mu, at, n_out),
        out_shape=jax.ShapeDtypeStruct((n_out, panel, width), BF),
        in_specs=[SMEM] + [ANY] * (1 + n_c),
        out_specs=ANY,
        scratch_shapes=[
            pltpu.VMEM(weighted.shape, BF),
            pltpu.VMEM((n_out, n_c, width, 128), BF),
            pltpu.VMEM((n_out, panel, width), BF),
            pltpu.SemaphoreType.DMA,
            pltpu.SemaphoreType.DMA((n_out, n_c)),
            pltpu.SemaphoreType.DMA((n_out,)),
        ],
        compiler_params=pltpu.CompilerParams(vmem_limit_bytes=VMEM_LIMIT),
        cost_estimate=pl.CostEstimate(
            flops=2 * panel * n_c * 128 * n_out * width, bytes_accessed=20 << 20, transcendentals=0
        ),
    )(tab, weighted, *pieces)


VM = pl.BlockSpec(memory_space=pltpu.VMEM)


def merge_kernel(i, half, first, base_ref, got_ref, out_ref, buf, sem):
    rows, quarter = buf.shape[0], got_ref.shape[0]
    copy = pltpu.make_async_copy(base_ref.at[i, pl.ds(half * rows, rows), :], buf, sem)
    copy.start()
    copy.wait()
    with_got = slice(0, quarter) if first else slice(quarter, 2 * quarter)
    without = slice(quarter, 2 * quarter) if first else slice(0, quarter)
    out_ref[without, :] = buf[without, :]
    out_ref[with_got, :] = (buf[with_got, :].astype(F32) + got_ref[...].astype(F32)).astype(BF)


def merge(base, got, i, half, first):
    rows, width = base.shape[1] // 2, base.shape[2]
    return pl.pallas_call(
        functools.partial(merge_kernel, i, half, first),
        in_specs=[ANY, VM],
        out_specs=VM,
        out_shape=jax.ShapeDtypeStruct((rows, width), BF),
        scratch_shapes=[pltpu.VMEM((rows, width), BF), pltpu.SemaphoreType.DMA],
        compiler_params=pltpu.CompilerParams(vmem_limit_bytes=8 << 20),
        cost_estimate=pl.CostEstimate(
            flops=rows * width * 64, bytes_accessed=rows * width * 4, transcendentals=0
        ),
    )(base, got)


def total_kernel(half, mu, tab, base_ref, below_ref, above_ref, sent_ref, kept_ref):
    rows = sent_ref.shape[0]
    part = slice(half * rows, (half + 1) * rows)
    for i, out in ((0, sent_ref), (1, kept_ref)):
        cols = pl.ds(pl.multiple_of(tab[AT_X + i] * mu, mu), mu)
        out[...] = (
            base_ref[0, part, cols].astype(F32)
            + below_ref[:, cols].astype(F32)
            + above_ref[:, cols].astype(F32)
        ).astype(out.dtype)


def totals(tab, base, below, above, half, mu):
    rows, width = below.shape
    return pl.pallas_call(
        functools.partial(total_kernel, half, mu),
        in_specs=[SMEM, VM, VM, VM],
        out_specs=(VM, VM),
        out_shape=(
            jax.ShapeDtypeStruct((rows, mu), BF),
            jax.ShapeDtypeStruct((rows, mu), F32),
        ),
        compiler_params=pltpu.CompilerParams(vmem_limit_bytes=8 << 20),
        cost_estimate=pl.CostEstimate(
            flops=rows * width * 64, bytes_accessed=rows * width * 8, transcendentals=0
        ),
    )(tab, base, below, above)


def pick_kernel(tab, c_ref, keep_ref, send_ref, buf, in_sem, out_sem):
    n, rows = 8, buf.shape[1] // 8

    def get(i, j):
        start = pl.multiple_of(tab[AT_ROWS + i * n + j] * rows, rows)
        return pltpu.make_async_copy(
            c_ref.at[pl.ds(start, rows), :], buf.at[i, pl.ds(j * rows, rows), :], in_sem.at[i, j]
        )

    for i in range(2):
        for j in range(n):
            get(i, j).start()
    for i, out in ((0, send_ref), (1, keep_ref)):
        for j in range(n):
            get(i, j).wait()
        pltpu.make_async_copy(buf.at[i], out, out_sem.at[i]).start()
    for i, out in ((0, send_ref), (1, keep_ref)):
        pltpu.make_async_copy(buf.at[i], out, out_sem.at[i]).wait()


def pick(tab, collocation):
    nbf, panel = collocation.shape
    block = jax.ShapeDtypeStruct((nbf // 2, panel), BF)
    return pl.pallas_call(
        pick_kernel,
        out_shape=(block, block),
        in_specs=[SMEM, ANY],
        out_specs=(ANY, ANY),
        scratch_shapes=[
            pltpu.VMEM((2, nbf // 2, panel), BF),
            pltpu.SemaphoreType.DMA((2, 8)),
            pltpu.SemaphoreType.DMA((2,)),
        ],
        cost_estimate=pl.CostEstimate(
            flops=1 << 30, bytes_accessed=4 * nbf * panel, transcendentals=0
        ),
        name="pick",
    )(tab, collocation)


def first_kernel(own_ref, par_ref, r_ref, rp_ref, o_ref):
    depth = r_ref.shape[0]
    o_ref[...] = jnp.dot(
        own_ref[:, :depth], r_ref[...], preferred_element_type=F32
    ) + jnp.dot(par_ref[:, :depth], rp_ref[...], preferred_element_type=F32)


def last_kernel(own_ref, par_ref, r_ref, rp_ref, acc_ref, *outs):
    rows, depth = outs[0].shape[0], r_ref.shape[0]
    for j, out in enumerate(outs):
        part = slice(j * rows, (j + 1) * rows)
        out[...] = (
            acc_ref[part, :]
            + jnp.dot(own_ref[part, depth:], r_ref[...], preferred_element_type=F32)
            + jnp.dot(par_ref[part, depth:], rp_ref[...], preferred_element_type=F32)
        ).astype(out.dtype)


def k_rows(own, par, red, red_par, acc=None):
    n, depth = own.shape[0], red.shape[0]
    mu = red.shape[1]
    cost = pl.CostEstimate(flops=4 * n * depth * mu, bytes_accessed=6 << 20, transcendentals=0)
    params = pltpu.CompilerParams(vmem_limit_bytes=16 << 20)
    if acc is None:
        return pl.pallas_call(
            first_kernel, in_specs=[VM] * 4, out_specs=VM, compiler_params=params,
            out_shape=jax.ShapeDtypeStruct((n, mu), F32), cost_estimate=cost, name="k_first",
        )(own, par, red, red_par)
    return pl.pallas_call(
        last_kernel, in_specs=[VM] * 5, out_specs=(VM,) * 8, compiler_params=params,
        out_shape=tuple(
            jax.ShapeDtypeStruct((n // 8, mu), F32 if j == 0 else BF) for j in range(8)
        ),
        cost_estimate=cost, name="k_last",
    )(own, par, red, red_par, acc)


def exchange(collocation, density, kernel):
    w = kernel.shape[3]
    gx = lax.axis_index("gx")
    gy = lax.axis_index("gy")
    core, y, xlo = gx & 1, (gx >> 1) & 3, gx >> 3
    z, xhi = gy >> 1, gy & 1
    sign = 1 - 2 * core
    mu = density.shape[0]

    own_piece = lax.dynamic_slice_in_dim(collocation, gy * w, w, 1)
    own_t = lax.dot_general(
        collocation, density, (((0,), (1,)), ((), ())), preferred_element_type=F32
    ).astype(BF)

    near = gx_perm(own_piece, YSPLIT)
    other = gx_perm(own_piece, CORE)
    piece_x = gx_perm(own_piece, XLO)
    near_other = gx_perm(other, YSPLIT)
    d_near = both_perm(own_t, ZSPLIT)
    d_other = gx_perm(own_t, CORE)
    d_near_other = both_perm(d_other, ZSPLIT)
    far = gx_perm(near, YSPLIT)
    own_x = gy_perm(own_t, XHI)
    d_far = both_perm(d_near, ZSPLIT)
    px = piece_x
    other_x = gx_perm(px, CORE)
    near_x = gx_perm(px, YSPLIT)
    near_other_x = gx_perm(other_x, YSPLIT)
    dx = own_x
    d_other_x = gx_perm(dx, CORE)
    d_near_x = both_perm(dx, ZSPLIT)
    d_near_other_x = both_perm(d_other_x, ZSPLIT)
    far_x = gx_perm(near_x, YSPLIT)
    d_far_x = both_perm(d_near_x, ZSPLIT)
    pieces = [
        own_piece, other, near, near_other,
        gx_perm(near_other, CORE), gx_perm(near, CORE),
        far, gx_perm(far, CORE),
        piece_x, other_x, near_x, near_other_x,
        gx_perm(near_other_x, CORE), gx_perm(near_x, CORE),
        far_x, gx_perm(far_x, CORE),
    ]
    blocks = [
        own_t, d_near, gx_perm(d_near_other, CORE), d_far,
        own_x, d_near_x, gx_perm(d_near_other_x, CORE), d_far_x,
    ]
    k_tab = []
    for xl in (xlo, 1 - xlo):
        for yy in (y, y - sign, y + sign, y + 2):
            for cc in (core, 1 - core):
                k_tab.append((xl * 4 + (yy & 3)) * 2 + cc)
    m_tab = []
    for h in (xhi, 1 - xhi):
        for zz in (z, z - sign, z + sign, z + 2):
            m_tab.append((zz & 3) * 2 + h)
    m_tab = [m_tab[j] for j in (0, 1, 2, 3, 4, 5, 7, 6)]

    tiles = jnp.transpose(after(kernel, near)[:, :, 0, :], (1, 0, 2))

    hops = [(dx, dy) for dx in (0, 1) for dy in range(4)]
    chips = [((xlo ^ dx) * 4 + ((y + dy) & 3)) * 2 for dx, dy in hops]
    tab = jnp.stack(
        m_tab + k_tab + [(z + 2) & 3, (z + 1) & 3, (z + 3) & 3, z]
        + [c + 1 - core for c in chips] + [c + core for c in chips] + [1 - xhi, xhi]
    ).astype(jnp.int32)
    blocks = [blocks[j] for j in (0, 1, 2, 3, 4, 5, 7, 6)]
    acc = early(tab, blocks[:6], pieces, mu)
    weighted, a1, a2, b1, b2 = weigh(tab, acc, tiles, blocks[6:], pieces, mu, 6)

    a1 = gy_perm(a1, ZUP)
    a2 = gy_perm(a2, ZDOWN)
    b1 = gy_perm(b1, ZUP)
    b2 = gy_perm(b2, ZDOWN)
    near_u = spread(tab, weighted, pieces, mu, AT_Z, 2)
    zero = spread(tab, weighted, pieces, mu, AT_Z + 2, 1)
    up_a = gy_perm(merge(near_u, a1, 0, 0, True), ZUP)
    down_a = gy_perm(merge(near_u, a2, 1, 0, False), ZDOWN)
    up_b = gy_perm(merge(near_u, b1, 0, 1, True), ZUP)
    down_b = gy_perm(merge(near_u, b2, 1, 1, False), ZDOWN)

    c_own, c_send = pick(tab, after(collocation, far))
    c_par = gx_perm(c_send, CORE)

    def finish(half, below, above):
        sent, kept = totals(tab, zero, below, above, half, mu)
        red = (kept + gy_perm(sent, XHI).astype(F32)).astype(BF)
        return red, gx_perm(red, CORE)

    part = k_rows(c_own, c_par, *finish(0, up_a, down_a))
    rows = k_rows(c_own, c_par, *finish(1, up_b, down_b), part)
    total = rows[0]
    for i in (6, 5, 7, 2, 1, 3, 4):
        dx, dy = hops[i]
        pairs = gx_pairs(lambda a, b, c, dx=dx, dy=dy: (a ^ dx, b + dy, c))
        total = total + gx_perm(rows[i], pairs).astype(F32)
    return total


def solution(mesh):
    return jax.shard_map(
        exchange,
        mesh=mesh,
        in_specs=(P(None, "gx"), P("gy", None), P("gx", None, "gy", None)),
        out_specs=P("gx", "gy"),
        check_vma=False,
    )
```

time: 360 us -> 244 us (0.68)
  blocking collectives: 114 us -> 0 us
  waiting for transfers between devices: 161 us -> 68.6 us
  starting transfers between devices: 0.04 us -> 82.3 us
  Pallas kernels: 0 us -> 70.7 us
  matrix products: 51 us -> 5.69 us
  between operations: 13.4 us -> 0.39 us
  other arithmetic: 11.6 us -> 1 us
  local copies, waits for them, and re-layouts: 8.69 us -> 14.9 us
    all_gather x2 -> x0, waiting for transfers between devices: 161 us -> none  [the longest x1 82.7 us: local(): dense_block = lax.all_gather(own_rows, 'gy', axis=0, tiled=True)]
    all_to_all x2 -> x0, blocking collectives: 114 us -> none  [summed_on_arrival(): lax.all_to_all(parts, axis, split_axis=0, concat_axis=0, tiled=True)]
    ppermute x0 -> x46, starting transfers between devices: none -> 82.3 us  [the longest x29 47.7 us: gx_perm(): return lax.ppermute(x, 'gx', pairs)]
    pallas_call x0 -> x13, Pallas kernels: none -> 70.7 us  [the longest x2 21 us: spread(): pl.pallas_call(functools.partial(spread_kernel, n_c, mu, at, n_out), out_...]
    ppermute x0 -> x46, waiting for transfers between devices: none -> 68.6 us  [the longest x11 29.9 us: gy_perm(): return lax.ppermute(x, 'gy', pairs)]
    dot_general x4 -> x1, matrix products: 51 us -> 5.69 us  [exchange(): lax.dot_general(collocation, density, (((0,), (1,)), ((), ())), preferred...]
    unnamed x1 -> x0, other arithmetic: 6.5 us -> none
    unnamed x4 -> x42, local copies, waits for them, and re-layouts: 1.67 us -> 7.79 us
  transfers between devices with their start and end apart: 2 -> 46, of which waited for: 2 -> 16; matrix products, arithmetic and copies ran while one was open for 2% -> 3% of each run, Pallas kernels for 0% -> 28%
where the time goes in v1:
time: 244 us
  starting transfers between devices  82.3 us (34%)
  Pallas kernels  70.7 us (29%)
  waiting for transfers between devices  68.6 us (28%)
  local copies, waits for them, and re-layouts  14.9 us (6%)
  matrix products  5.69 us (2%)
    ppermute x29, starting transfers between devices, gx_perm(): return lax.ppermute(x, 'gx', pairs)  47.7 us
    ppermute x11, waiting for transfers between devices, gy_perm(): return lax.ppermute(x, 'gy', pairs)  29.9 us
    ppermute x29, waiting for transfers between devices, gx_perm(): return lax.ppermute(x, 'gx', pairs)  28.3 us
    pallas_call x2, Pallas kernels, spread(): pl.pallas_call(functools.partial(spread_kernel, n_c, mu, at, n_out), out_...  21 us
    ppermute x11, starting transfers between devices, gy_perm(): return lax.ppermute(x, 'gy', pairs)  18.5 us
    pallas_call x1, Pallas kernels, early(): pl.pallas_call(functools.partial(early_kernel, n_d, n_c, mu), out_shape=j...  16.5 us
    ppermute x6, starting transfers between devices, both_perm(): return lax.ppermute(x, ('gx', 'gy'), pairs)  16.2 us
    pallas_call x1, Pallas kernels, weigh(): pl.pallas_call(functools.partial(weigh_kernel, n_d, n_c, mu, first), out_...  13.9 us
  transfers between devices with their start and end apart: 46, of which 16 were waited for; matrix products, arithmetic and copies ran while one was open for 3% of the time, Pallas kernels for 28%

profile of v1, /device:TPU:1, one launch (start us, length us, event | category | flops | bytes accessed | tf_op | source)
XLA Modules:
  0.0 243.5 jit_solution(3387769387286735717)
XLA Ops:
  1.7 5.7 %convolution_convert_fusion.refs_0_ = bf16[1024,384]{1,0:T(8,128)(2,1)S(1)} fusion(bf16[3072,1024]{1,0:T(8,128)(2,1)} %c_ref, bf16[384,3072]{1,0:T(8,128)(2,1)S(1)} %copy-done), kind=kOutput, calls=%fused_computation.1 | convolution fusion | flops 2416312320 | bytes 9437184 | tf_op jit(solution)/shard_map/dot_general | solution.py:473
  7.4 3.7 %collective-permute-start.8 = (bf16[1024,384]{1,0:T(8,128)(2,1)S(1)}, bf16[1024,384]{1,0:T(8,128)(2,1)}, u32[]{:S(2)}, u32[]{:S(2)}) collective-permute-start(bf16[1024,384]{1,0:T(8,128)(2,1)S(1)} %convolution_convert_fusion.refs_0_), channel_id=1, source_target_pairs={{0,1},{1,0},{2,3},{3,2},{4,5},{5,4},{6,7},{7,6},{8,9},{9,8},{10,11... | collective-permute-start | bytes 2359304 | tf_op jit(solution)/shard_map/ppermute | solution.py:62
  12.0 3.8 %collective-permute-start.3 = (bf16[1024,384]{1,0:T(8,128)(2,1)S(1)}, bf16[1024,384]{1,0:T(8,128)(2,1)}, u32[]{:S(2)}, u32[]{:S(2)}) collective-permute-start(bf16[1024,384]{1,0:T(8,128)(2,1)S(1)} %convolution_convert_fusion.refs_0_), channel_id=1, source_target_pairs={{0,2},{1,3},{2,4},{3,5},{4,6},{5,7},{6,0},{7,1},{8,14},{9,15},{10,... | collective-permute-start | bytes 2359304 | tf_op jit(solution)/shard_map/ppermute | solution.py:66
  17.3 10.7 %collective-permute-done.8.refs_4_ = bf16[1024,384]{1,0:T(8,128)(2,1)} collective-permute-done((bf16[1024,384]{1,0:T(8,128)(2,1)S(1)}, bf16[1024,384]{1,0:T(8,128)(2,1)}, u32[]{:S(2)}, u32[]{:S(2)}) %collective-permute-start.8) | collective-permute-done | bytes 786464 | tf_op jit(solution)/shard_map/ppermute | solution.py:62
  32.6 3.8 %collective-permute-start.9 = (bf16[1024,384]{1,0:T(8,128)(2,1)}, bf16[1024,384]{1,0:T(8,128)(2,1)S(1)}, u32[]{:S(2)}, u32[]{:S(2)}) collective-permute-start(bf16[1024,384]{1,0:T(8,128)(2,1)} %collective-permute-done.8.refs_4_), channel_id=1, source_target_pairs={{0,2},{1,3},{2,4},{3,5},{4,6},{5,7},{6,0},{7,1},{8,14},{9,15},{10,... | collective-permute-start | bytes 2359304 | tf_op jit(solution)/shard_map/ppermute | solution.py:66
  36.3 8.8 %collective-permute-done.15.refs_14_.refs_12_.refs_9_ = bf16[3072,128]{1,0:T(8,128)(2,1)S(1)} collective-permute-done((bf16[3072,128]{1,0:T(8,128)(2,1)S(1)}, bf16[3072,128]{1,0:T(8,128)(2,1)S(1)}, u32[]{:S(2)}, u32[]{:S(2)}) %collective-permute-start.15) | collective-permute-done | bytes 786464 | tf_op jit(solution)/shard_map/ppermute | solution.py:58
  45.1 3.8 %collective-permute-start.5 = (bf16[1024,384]{1,0:T(8,128)(2,1)}, bf16[1024,384]{1,0:T(8,128)(2,1)S(1)}, u32[]{:S(2)}, u32[]{:S(2)}) collective-permute-start(bf16[1024,384]{1,0:T(8,128)(2,1)} %collective-permute-done.4), channel_id=1, source_target_pairs={{0,2},{1,3},{2,4},{3,5},{4,6},{5,7},{6,0},{7,1},{8,14},{9,15},{10,... | collective-permute-start | bytes 2359304 | tf_op jit(solution)/shard_map/ppermute | solution.py:66
  53.5 4.7 %collective-permute-done.5 = bf16[1024,384]{1,0:T(8,128)(2,1)S(1)} collective-permute-done((bf16[1024,384]{1,0:T(8,128)(2,1)}, bf16[1024,384]{1,0:T(8,128)(2,1)S(1)}, u32[]{:S(2)}, u32[]{:S(2)}) %collective-permute-start.5) | collective-permute-done | bytes 786464 | tf_op jit(solution)/shard_map/ppermute | solution.py:66
  60.9 5.7 %collective-permute-done.7.refs_3_ = bf16[1024,384]{1,0:T(8,128)(2,1)S(1)} collective-permute-done((bf16[1024,384]{1,0:T(8,128)(2,1)}, bf16[1024,384]{1,0:T(8,128)(2,1)S(1)}, u32[]{:S(2)}, u32[]{:S(2)}) %collective-permute-start.7) | collective-permute-done | bytes 786464 | tf_op jit(solution)/shard_map/ppermute | solution.py:66
  73.9 4.3 %collective-permute-done.1.refs_12_.refs_10_.refs_7_ = bf16[3072,128]{1,0:T(8,128)(2,1)} collective-permute-done((bf16[3072,128]{1,0:T(8,128)(2,1)S(1)}, bf16[3072,128]{1,0:T(8,128)(2,1)}, u32[]{:S(2)}, u32[]{:S(2)}) %collective-permute-start.1) | collective-permute-done | bytes 786464 | tf_op jit(solution)/shard_map/ppermute | solution.py:58
  78.2 4.4 %collective-permute-start.20 = (bf16[3072,128]{1,0:T(8,128)(2,1)S(1)}, bf16[3072,128]{1,0:T(8,128)(2,1)}, u32[]{:S(2)}, u32[]{:S(2)}) collective-permute-start(bf16[3072,128]{1,0:T(8,128)(2,1)S(1)} %collective-permute-done.17.refs_16_.refs_14_.refs_11_), channel_id=1, source_target_pairs={{0,8},{8,0},{16,24},{24,16},{32,40},{40,32},{48,56},{56,48},{64,72... | collective-permute-start | bytes 2359304 | tf_op jit(solution)/shard_map/ppermute | solution.py:58
  86.7 4.4 %collective-permute-start.22 = (bf16[3072,128]{1,0:T(8,128)(2,1)}, bf16[3072,128]{1,0:T(8,128)(2,1)}, u32[]{:S(2)}, u32[]{:S(2)}) collective-permute-start(bf16[3072,128]{1,0:T(8,128)(2,1)} %collective-permute-done.21.refs_20_.refs_18_.refs_15_), channel_id=1, source_target_pairs={{0,8},{8,0},{16,24},{24,16},{32,40},{40,32},{48,56},{56,48},{64,72... | collective-permute-start | bytes 2359304 | tf_op jit(solution)/shard_map/ppermute | solution.py:58
  91.1 4.0 %collective-permute-done.18.refs_17_.refs_15_.refs_12_ = bf16[3072,128]{1,0:T(8,128)(2,1)} collective-permute-done((bf16[3072,128]{1,0:T(8,128)(2,1)S(1)}, bf16[3072,128]{1,0:T(8,128)(2,1)}, u32[]{:S(2)}, u32[]{:S(2)}) %collective-permute-start.18) | collective-permute-done | bytes 786464 | tf_op jit(solution)/shard_map/ppermute | solution.py:58
  95.1 4.5 %collective-permute-start.19 = (bf16[3072,128]{1,0:T(8,128)(2,1)}, bf16[3072,128]{1,0:T(8,128)(2,1)}, u32[]{:S(2)}, u32[]{:S(2)}) collective-permute-start(bf16[3072,128]{1,0:T(8,128)(2,1)} %collective-permute-done.18.refs_17_.refs_15_.refs_12_), channel_id=1, source_target_pairs={{0,8},{8,0},{16,24},{24,16},{32,40},{40,32},{48,56},{56,48},{64,72... | collective-permute-start | bytes 2359304 | tf_op jit(solution)/shard_map/ppermute | solution.py:58
  100.2 5.3 %copy.6 = bf16[1024,16,1,128]{3,0,1,2:T(8,128)(2,1)} copy(bf16[1024,16,1,128]{3,1,2,0:T(8,128)(2,1)} %param.5) | data formatting | bytes 8388608 | tf_op jit(solution)/shard_map/optimization_barrier | solution.py:70
  105.5 5.3 %pick.1 = (bf16[1536,1024]{1,0:T(8,128)(2,1)}, bf16[1536,1024]{1,0:T(8,128)(2,1)}) custom-call(s32[46]{0:T(128)} %stack.181.tab, bf16[3072,1024]{1,0:T(8,128)(2,1)} %c_ref), custom_call_target="tpu_custom_call" | custom-call | flops 1073741824 | bytes 12582912 | tf_op jit(solution)/shard_map/pick/pallas_call | solution.py:409
  112.8 16.5 %early.1.refs_0_ = bf16[8,1024,256]{2,1,0:T(8,128)(2,1)} custom-call(s32[46]{0:T(128)} %stack.181.tab, bf16[1024,384]{1,0:T(8,128)(2,1)} %copy-done.15, bf16[1024,384]{1,0:T(8,128)(2,1)} %collective-permute-done.3.refs_1_, bf16[1024,384]{1,0:T(8,128)(2,1)} %copy-done.19, bf16[1024,384]{1,0:T(8,128)(2,1)} %copy-done.17, ...), custom_call_target="tpu_custom_call" | custom-call | flops 9663676416 | bytes 25165824 | tf_op jit(solution)/shard_map/early/pallas_call | solution.py:128
  130.2 13.9 %weigh.1 = (bf16[8,1024,256]{2,1,0:T(8,128)(2,1)}, bf16[256,768]{1,0:T(8,128)(2,1)}, bf16[256,768]{1,0:T(8,128)(2,1)}, bf16[256,768]{1,0:T(8,128)(2,1)}, bf16[256,768]{1,0:T(8,128)(2,1)}) custom-call(s32[46]{0:T(128)} %stack.181.tab, bf16[8,1024,256]{2,1,0:T(8,128)(2,1)} %early.1.refs_0_, bf16[16,1024,128]{2,1,0:T(8,128)(2,1)} %bitcast.51, ...), custom_call_target="tpu_custom_call" | custom-call | flops 6442450944 | bytes 25165824 | tf_op jit(solution)/shard_map/weigh/pallas_call | solution.py:242
  149.5 12.3 %shard_map.38.base_ref = bf16[2,1024,768]{2,1,0:T(8,128)(2,1)} custom-call(s32[46]{0:T(128)} %stack.181.tab, bf16[8,1024,256]{2,1,0:T(8,128)(2,1)} %get-tuple-element.30.refs_0_, bf16[3072,128]{1,0:T(8,128)(2,1)} %copy-done.8, bf16[3072,128]{1,0:T(8,128)(2,1)} %copy-done.10, bf16[3072,128]{1,0:T(8,128)(2,1)} %copy-done.11, ...), custom_call_target="tpu_custom_call" | custom-call | flops 6442450944 | bytes 20971520 | tf_op jit(solution)/shard_map/pallas_call | solution.py:308
  179.2 8.7 %shard_map.37.base_ref = bf16[1,1024,768]{2,1,0:T(8,128)(2,1)} custom-call(s32[46]{0:T(128)} %stack.181.tab, bf16[8,1024,256]{2,1,0:T(8,128)(2,1)} %get-tuple-element.30.refs_0_, bf16[3072,128]{1,0:T(8,128)(2,1)} %copy-done.8, bf16[3072,128]{1,0:T(8,128)(2,1)} %copy-done.10, bf16[3072,128]{1,0:T(8,128)(2,1)} %copy-done.11, ...), custom_call_target="tpu_custom_call" | custom-call | flops 3221225472 | bytes 20971520 | tf_op jit(solution)/shard_map/pallas_call | solution.py:308
  192.7 10.6 %collective-permute-done.28.below_ref = bf16[512,768]{1,0:T(8,128)(2,1)} collective-permute-done((bf16[512,768]{1,0:T(8,128)(2,1)}, bf16[512,768]{1,0:T(8,128)(2,1)}, u32[]{:S(2)}, u32[]{:S(2)}) %collective-permute-start.28) | collective-permute-done | bytes 786464 | tf_op jit(solution)/shard_map/ppermute | solution.py:62
  210.8 5.1 %collective-permute-done.31 = bf16[512,384]{1,0:T(8,128)(2,1)S(1)} collective-permute-done((bf16[512,384]{1,0:T(8,128)(2,1)S(1)}, bf16[512,384]{1,0:T(8,128)(2,1)S(1)}, u32[]{:S(2)}, u32[]{:S(2)}) %collective-permute-start.31) | collective-permute-done | bytes 393248 | tf_op jit(solution)/shard_map/ppermute | solution.py:62
  216.0 3.4 %collective-permute-start.32 = (bf16[512,384]{1,0:T(8,128)(2,1)S(1)}, bf16[512,384]{1,0:T(8,128)(2,1)S(1)}, u32[]{:S(2)}, u32[]{:S(2)}) collective-permute-start(bf16[512,384]{1,0:T(8,128)(2,1)S(1)} %add_convert_fusion.1.r_ref), channel_id=1, source_target_pairs={{0,8},{8,0},{16,24},{24,16},{32,40},{40,32},{48,56},{56,48},{64,72... | collective-permute-start | bytes 1179656 | tf_op jit(solution)/shard_map/ppermute | solution.py:58
  239.2 3.4 %collective-permute-done.43 = bf16[192,384]{1,0:T(8,128)(2,1)S(1)} collective-permute-done((bf16[192,384]{1,0:T(8,128)(2,1)S(1)}, bf16[192,384]{1,0:T(8,128)(2,1)S(1)}, u32[]{:S(2)}, u32[]{:S(2)}) %collective-permute-start.43) | collective-permute-done | bytes 147488 | tf_op jit(solution)/shard_map/ppermute | solution.py:58
  (130 shorter events, 86.6 us)
Async XLA Ops:
  7.4 20.6 %collective-permute-start.8 = (bf16[1024,384]{1,0:T(8,128)(2,1)S(1)}, bf16[1024,384]{1,0:T(8,128)(2,1)}, u32[]{:S(2)}, u32[]{:S(2)}) collective-permute-start(bf16[1024,384]{1,0:T(8,128)(2,1)S(1)} %convolution_convert_fusion.refs_0_), channel_id=1, source_target_pairs={{0,1},{1,0},{2,3},{3,2},{4,5},{5,4},{6,7},{7,6},{8,9},{9,8},{10,11... | collective-permute-start | bytes 2359304 | tf_op jit(solution)/shard_map/ppermute | solution.py:62
  11.0 20.0 %collective-permute-start.4 = (bf16[1024,384]{1,0:T(8,128)(2,1)S(1)}, bf16[1024,384]{1,0:T(8,128)(2,1)}, u32[]{:S(2)}, u32[]{:S(2)}) collective-permute-start(bf16[1024,384]{1,0:T(8,128)(2,1)S(1)} %convolution_convert_fusion.refs_0_), channel_id=1, source_target_pairs={{0,8},{8,0},{16,24},{24,16},{32,40},{40,32},{48,56},{56,48},{64,72... | collective-permute-start | bytes 2359304 | tf_op jit(solution)/shard_map/ppermute | solution.py:58
  12.0 20.6 %collective-permute-start.3 = (bf16[1024,384]{1,0:T(8,128)(2,1)S(1)}, bf16[1024,384]{1,0:T(8,128)(2,1)}, u32[]{:S(2)}, u32[]{:S(2)}) collective-permute-start(bf16[1024,384]{1,0:T(8,128)(2,1)S(1)} %convolution_convert_fusion.refs_0_), channel_id=1, source_target_pairs={{0,2},{1,3},{2,4},{3,5},{4,6},{5,7},{6,0},{7,1},{8,14},{9,15},{10,... | collective-permute-start | bytes 2359304 | tf_op jit(solution)/shard_map/ppermute | solution.py:66
  16.9 28.2 %collective-permute-start.15 = (bf16[3072,128]{1,0:T(8,128)(2,1)S(1)}, bf16[3072,128]{1,0:T(8,128)(2,1)S(1)}, u32[]{:S(2)}, u32[]{:S(2)}) collective-permute-start(bf16[3072,128]{1,0:T(8,128)(2,1)S(1)} %constant_dynamic-slice_fusion.refs_6_.refs_4_.refs_1_), channel_id=1, source_target_pairs={{0,64},{8,72},{16,80},{24,88},{32,96},{40,104},{48,112},{56,120},{... | collective-permute-start | bytes 2359304 | tf_op jit(solution)/shard_map/ppermute | solution.py:58
  17.3 31.6 %collective-permute-start.10 = (bf16[3072,128]{1,0:T(8,128)(2,1)S(1)}, bf16[3072,128]{1,0:T(8,128)(2,1)S(1)}, u32[]{:S(2)}, u32[]{:S(2)}) collective-permute-start(bf16[3072,128]{1,0:T(8,128)(2,1)S(1)} %constant_dynamic-slice_fusion.refs_6_.refs_4_.refs_1_), channel_id=1, source_target_pairs={{0,8},{8,0},{16,24},{24,16},{32,40},{40,32},{48,56},{56,48},{64,72... | collective-permute-start | bytes 2359304 | tf_op jit(solution)/shard_map/ppermute | solution.py:58
  28.0 21.0 %collective-permute-start = (bf16[3072,128]{1,0:T(8,128)(2,1)S(1)}, bf16[3072,128]{1,0:T(8,128)(2,1)S(1)}, u32[]{:S(2)}, u32[]{:S(2)}) collective-permute-start(bf16[3072,128]{1,0:T(8,128)(2,1)S(1)} %constant_dynamic-slice_fusion.refs_6_.refs_4_.refs_1_), channel_id=1, source_target_pairs={{0,16},{8,56},{16,32},{24,8},{32,48},{40,24},{48,0},{56,40},{64,80... | collective-permute-start | bytes 2359304 | tf_op jit(solution)/shard_map/ppermute | solution.py:58
  31.1 20.7 %collective-permute-start.24 = (bf16[1024,384]{1,0:T(8,128)(2,1)}, bf16[1024,384]{1,0:T(8,128)(2,1)S(1)}, u32[]{:S(2)}, u32[]{:S(2)}) collective-permute-start(bf16[1024,384]{1,0:T(8,128)(2,1)} %collective-permute-done.8.refs_4_), channel_id=1, source_target_pairs={{0,8},{8,0},{16,24},{24,16},{32,40},{40,32},{48,56},{56,48},{64,72... | collective-permute-start | bytes 2359304 | tf_op jit(solution)/shard_map/ppermute | solution.py:58
  32.6 19.6 %collective-permute-start.9 = (bf16[1024,384]{1,0:T(8,128)(2,1)}, bf16[1024,384]{1,0:T(8,128)(2,1)S(1)}, u32[]{:S(2)}, u32[]{:S(2)}) collective-permute-start(bf16[1024,384]{1,0:T(8,128)(2,1)} %collective-permute-done.8.refs_4_), channel_id=1, source_target_pairs={{0,2},{1,3},{2,4},{3,5},{4,6},{5,7},{6,0},{7,1},{8,14},{9,15},{10,... | collective-permute-start | bytes 2359304 | tf_op jit(solution)/shard_map/ppermute | solution.py:66
  49.0 20.3 %collective-permute-start.17 = (bf16[3072,128]{1,0:T(8,128)(2,1)S(1)}, bf16[3072,128]{1,0:T(8,128)(2,1)S(1)}, u32[]{:S(2)}, u32[]{:S(2)}) collective-permute-start(bf16[3072,128]{1,0:T(8,128)(2,1)S(1)} %collective-permute-done.15.refs_14_.refs_12_.refs_9_), channel_id=1, source_target_pairs={{0,16},{8,56},{16,32},{24,8},{32,48},{40,24},{48,0},{56,40},{64,80... | collective-permute-start | bytes 2359304 | tf_op jit(solution)/shard_map/ppermute | solution.py:58
  51.8 20.5 %collective-permute-start.16 = (bf16[3072,128]{1,0:T(8,128)(2,1)S(1)}, bf16[3072,128]{1,0:T(8,128)(2,1)S(1)}, u32[]{:S(2)}, u32[]{:S(2)}) collective-permute-start(bf16[3072,128]{1,0:T(8,128)(2,1)S(1)} %collective-permute-done.15.refs_14_.refs_12_.refs_9_), channel_id=1, source_target_pairs={{0,8},{8,0},{16,24},{24,16},{32,40},{40,32},{48,56},{56,48},{64,72... | collective-permute-start | bytes 2359304 | tf_op jit(solution)/shard_map/ppermute | solution.py:58
  52.1 20.3 %collective-permute-start.11 = (bf16[3072,128]{1,0:T(8,128)(2,1)S(1)}, bf16[3072,128]{1,0:T(8,128)(2,1)}, u32[]{:S(2)}, u32[]{:S(2)}) collective-permute-start(bf16[3072,128]{1,0:T(8,128)(2,1)S(1)} %collective-permute-done.10.refs_7_.refs_5_.refs_2_), channel_id=1, source_target_pairs={{0,16},{8,56},{16,32},{24,8},{32,48},{40,24},{48,0},{56,40},{64,80... | collective-permute-start | bytes 2359304 | tf_op jit(solution)/shard_map/ppermute | solution.py:58
  73.0 22.1 %collective-permute-start.18 = (bf16[3072,128]{1,0:T(8,128)(2,1)S(1)}, bf16[3072,128]{1,0:T(8,128)(2,1)}, u32[]{:S(2)}, u32[]{:S(2)}) collective-permute-start(bf16[3072,128]{1,0:T(8,128)(2,1)S(1)} %collective-permute-done.16.refs_15_.refs_13_.refs_10_), channel_id=1, source_target_pairs={{0,16},{8,56},{16,32},{24,8},{32,48},{40,24},{48,0},{56,40},{64,80... | collective-permute-start | bytes 2359304 | tf_op jit(solution)/shard_map/ppermute | solution.py:58
  78.2 32.6 %collective-permute-start.20 = (bf16[3072,128]{1,0:T(8,128)(2,1)S(1)}, bf16[3072,128]{1,0:T(8,128)(2,1)}, u32[]{:S(2)}, u32[]{:S(2)}) collective-permute-start(bf16[3072,128]{1,0:T(8,128)(2,1)S(1)} %collective-permute-done.17.refs_16_.refs_14_.refs_11_), channel_id=1, source_target_pairs={{0,8},{8,0},{16,24},{24,16},{32,40},{40,32},{48,56},{56,48},{64,72... | collective-permute-start | bytes 2359304 | tf_op jit(solution)/shard_map/ppermute | solution.py:58
  82.6 28.3 %collective-permute-start.12 = (bf16[3072,128]{1,0:T(8,128)(2,1)}, bf16[3072,128]{1,0:T(8,128)(2,1)}, u32[]{:S(2)}, u32[]{:S(2)}) collective-permute-start(bf16[3072,128]{1,0:T(8,128)(2,1)} %collective-permute-done.11.refs_9_.refs_7_.refs_4_), channel_id=1, source_target_pairs={{0,8},{8,0},{16,24},{24,16},{32,40},{40,32},{48,56},{56,48},{64,72... | collective-permute-start | bytes 2359304 | tf_op jit(solution)/shard_map/ppermute | solution.py:58
  84.1 28.6 %collective-permute-start.14 = (bf16[3072,128]{1,0:T(8,128)(2,1)}, bf16[3072,128]{1,0:T(8,128)(2,1)}, u32[]{:S(2)}, u32[]{:S(2)}) collective-permute-start(bf16[3072,128]{1,0:T(8,128)(2,1)} %collective-permute-done.1.refs_12_.refs_10_.refs_7_), channel_id=1, source_target_pairs={{0,8},{8,0},{16,24},{24,16},{32,40},{40,32},{48,56},{56,48},{64,72... | collective-permute-start | bytes 2359304 | tf_op jit(solution)/shard_map/ppermute | solution.py:58
  86.7 26.1 %collective-permute-start.22 = (bf16[3072,128]{1,0:T(8,128)(2,1)}, bf16[3072,128]{1,0:T(8,128)(2,1)}, u32[]{:S(2)}, u32[]{:S(2)}) collective-permute-start(bf16[3072,128]{1,0:T(8,128)(2,1)} %collective-permute-done.21.refs_20_.refs_18_.refs_15_), channel_id=1, source_target_pairs={{0,8},{8,0},{16,24},{24,16},{32,40},{40,32},{48,56},{56,48},{64,72... | collective-permute-start | bytes 2359304 | tf_op jit(solution)/shard_map/ppermute | solution.py:58
  110.8 108.5 %collective-permute-start.2 = (bf16[1536,1024]{1,0:T(8,128)(2,1)}, bf16[1536,1024]{1,0:T(8,128)(2,1)S(1)}, u32[]{:S(2)}, u32[]{:S(2)}) collective-permute-start(bf16[1536,1024]{1,0:T(8,128)(2,1)} %get-tuple-element.28), channel_id=1, source_target_pairs={{0,8},{8,0},{16,24},{24,16},{32,40},{40,32},{48,56},{56,48},{64,72... | collective-permute-start | bytes 9437192 | tf_op jit(solution)/shard_map/ppermute | solution.py:58
  144.0 28.0 %collective-permute-start.27 = (bf16[256,768]{1,0:T(8,128)(2,1)}, bf16[256,768]{1,0:T(8,128)(2,1)}, u32[]{:S(2)}, u32[]{:S(2)}) collective-permute-start(bf16[256,768]{1,0:T(8,128)(2,1)} %get-tuple-element.31), channel_id=1, source_target_pairs={{0,2},{1,3},{2,4},{3,5},{4,6},{5,7},{6,0},{7,1},{8,10},{9,11},{10,... | collective-permute-start | bytes 1179656 | tf_op jit(solution)/shard_map/ppermute | solution.py:62
  144.3 29.9 %collective-permute-start.29 = (bf16[256,768]{1,0:T(8,128)(2,1)}, bf16[256,768]{1,0:T(8,128)(2,1)}, u32[]{:S(2)}, u32[]{:S(2)}) collective-permute-start(bf16[256,768]{1,0:T(8,128)(2,1)} %get-tuple-element.32), channel_id=1, source_target_pairs={{0,6},{1,7},{2,0},{3,1},{4,2},{5,3},{6,4},{7,5},{8,14},{9,15},{10,... | collective-permute-start | bytes 1179656 | tf_op jit(solution)/shard_map/ppermute | solution.py:62
  146.8 20.4 %collective-permute-start.35 = (bf16[256,768]{1,0:T(8,128)(2,1)}, bf16[256,768]{1,0:T(8,128)(2,1)}, u32[]{:S(2)}, u32[]{:S(2)}) collective-permute-start(bf16[256,768]{1,0:T(8,128)(2,1)} %get-tuple-element.36), channel_id=1, source_target_pairs={{0,6},{1,7},{2,0},{3,1},{4,2},{5,3},{6,4},{7,5},{8,14},{9,15},{10,... | collective-permute-start | bytes 1179656 | tf_op jit(solution)/shard_map/ppermute | solution.py:62
  167.1 20.9 %collective-permute-start.34 = (bf16[512,768]{1,0:T(8,128)(2,1)}, bf16[512,768]{1,0:T(8,128)(2,1)S(1)}, u32[]{:S(2)}, u32[]{:S(2)}) collective-permute-start(bf16[512,768]{1,0:T(8,128)(2,1)} %shard_map.42), channel_id=1, source_target_pairs={{0,2},{1,3},{2,4},{3,5},{4,6},{5,7},{6,0},{7,1},{8,10},{9,11},{10,... | collective-permute-start | bytes 2359304 | tf_op jit(solution)/shard_map/ppermute | solution.py:62
  169.3 18.7 %collective-permute-start.36 = (bf16[512,768]{1,0:T(8,128)(2,1)}, bf16[512,768]{1,0:T(8,128)(2,1)}, u32[]{:S(2)}, u32[]{:S(2)}) collective-permute-start(bf16[512,768]{1,0:T(8,128)(2,1)} %shard_map.43), channel_id=1, source_target_pairs={{0,6},{1,7},{2,0},{3,1},{4,2},{5,3},{6,4},{7,5},{8,14},{9,15},{10,... | collective-permute-start | bytes 2359304 | tf_op jit(solution)/shard_map/ppermute | solution.py:62
  174.1 29.2 %collective-permute-start.28 = (bf16[512,768]{1,0:T(8,128)(2,1)}, bf16[512,768]{1,0:T(8,128)(2,1)}, u32[]{:S(2)}, u32[]{:S(2)}) collective-permute-start(bf16[512,768]{1,0:T(8,128)(2,1)} %shard_map.39), channel_id=1, source_target_pairs={{0,2},{1,3},{2,4},{3,5},{4,6},{5,7},{6,0},{7,1},{8,10},{9,11},{10,... | collective-permute-start | bytes 2359304 | tf_op jit(solution)/shard_map/ppermute | solution.py:62
  176.3 28.1 %collective-permute-start.30 = (bf16[512,768]{1,0:T(8,128)(2,1)}, bf16[512,768]{1,0:T(8,128)(2,1)}, u32[]{:S(2)}, u32[]{:S(2)}) collective-permute-start(bf16[512,768]{1,0:T(8,128)(2,1)} %shard_map.40), channel_id=1, source_target_pairs={{0,6},{1,7},{2,0},{3,1},{4,2},{5,3},{6,4},{7,5},{8,14},{9,15},{10,... | collective-permute-start | bytes 2359304 | tf_op jit(solution)/shard_map/ppermute | solution.py:62
  (43 other events, 728.5 us)

commit v2 on v1

--- a/solution.py
+++ b/solution.py
@@ -12,8 +12,8 @@
 F32 = jnp.float32
 ANY = pl.BlockSpec(memory_space=pl.ANY)
 SMEM = pl.BlockSpec(memory_space=pltpu.SMEM)
-VMEM_LIMIT = 60 * 1024 * 1024
-AT_Z, AT_ROWS, AT_X = 25, 28, 44
+VM = pl.BlockSpec(memory_space=pltpu.VMEM)
+AT_OWN, AT_OTHER, AT_ROWS = 24, 28, 32
 
 
 def gx_pairs(f):
@@ -138,7 +138,7 @@
             pltpu.SemaphoreType.DMA((n_c, n_d)),
             pltpu.SemaphoreType.DMA((n_c // 2,)),
         ],
-        compiler_params=pltpu.CompilerParams(vmem_limit_bytes=VMEM_LIMIT),
+        compiler_params=pltpu.CompilerParams(vmem_limit_bytes=60 << 20),
         cost_estimate=pl.CostEstimate(
             flops=2 * panel * n_c * 128 * n_d * mu, bytes_accessed=24 << 20, transcendentals=0
         ),
@@ -146,15 +146,31 @@
     )(tab, *blocks, *pieces)
 
 
+def u_parts(w_ref, c_s, first_row, mu, outs):
+    u = lax.dot_general(
+        lanes(w_ref, 0, w_ref.shape[0]),
+        lanes(c_s, 0, c_s.shape[0], slice(first_row, first_row + 2 * mu)),
+        (((1,), (1,)), ((), ())), preferred_element_type=F32,
+    ).astype(BF)
+    half = u.shape[0] // 2
+    a_refs, own_ref, other_ref = outs[:-2], outs[-2], outs[-1]
+    rows = half // len(a_refs)
+    for i, ref in enumerate(a_refs):
+        ref[...] = u[i * rows : (i + 1) * rows]
+    own_ref[...] = u[half:, :mu]
+    other_ref[...] = u[half:, mu:]
+
+
+def u_shapes(half, mu, parts):
+    a = (jax.ShapeDtypeStruct((half // parts, 2 * mu), BF),) * parts
+    return a + (jax.ShapeDtypeStruct((half, mu), BF),) * 2
+
+
 def weigh_kernel(n_d, n_c, mu, first, tab, *refs):
     acc_ref, z_ref = refs[:2]
     d_refs, c_refs = refs[2 : 2 + n_d], refs[2 + n_d : 2 + n_d + n_c]
-    outs = refs[2 + n_d + n_c : 7 + n_d + n_c]
-    w_out, u_outs = outs[0], outs[1:]
-    d_s, c_s, f_s, z_s, w_s, u_s, d_sem, c_sem, f_sem, z_sem, a_sem, o_sem, u_sem = refs[
-        7 + n_d + n_c :
-    ]
-    width = 2 * mu
+    outs = refs[2 + n_d + n_c : 10 + n_d + n_c]
+    d_s, c_s, f_s, z_s, w_s, d_sem, c_sem, f_sem, z_sem, a_sem, o_sem = refs[10 + n_d + n_c :]
     tiles = n_c // 2
 
     def c_copy(ref, p, j, rows):
@@ -168,15 +184,15 @@
     def acc_copy(q):
         return pltpu.make_async_copy(acc_ref.at[q], w_s.at[q], a_sem.at[q])
 
-    def far_copy(p):
-        rows = pl.multiple_of(tab[24] * width, width)
-        return pltpu.make_async_copy(c_refs[p].at[pl.ds(rows, width), :], f_s.at[p], f_sem.at[p])
+    def far_copy(p, i):
+        place = tab[(AT_OWN, AT_OTHER)[i % 2] + i // 2]
+        return pltpu.make_async_copy(
+            c_refs[p].at[pl.ds(pl.multiple_of(place * mu, mu), mu), :],
+            f_s.at[p, pl.ds(i * mu, mu), :], f_sem.at[p, i],
+        )
 
     def w_copy(q):
-        return pltpu.make_async_copy(w_s.at[q], w_out.at[q], o_sem.at[q])
-
-    for j in range(n_d):
-        pltpu.make_async_copy(d_refs[j], d_s.at[j], d_sem.at[j]).start()
+        return pltpu.make_async_copy(w_s.at[q], outs[0].at[q], o_sem.at[q])
 
     def fetch(q):
         for p in (2 * q, 2 * q + 1):
@@ -187,8 +203,11 @@
 
     def fetch_far(q):
         for p in (2 * q, 2 * q + 1):
-            far_copy(p).start()
-
+            for i in range(4):
+                far_copy(p, i).start()
+
+    for j in range(n_d):
+        pltpu.make_async_copy(d_refs[j], d_s.at[j], d_sem.at[j]).start()
     for q in range(2):
         fetch(q)
     for j in range(n_d):
@@ -213,174 +232,142 @@
 
     lax.fori_loop(0, tiles, tile, 0)
     for p in range(n_c):
-        far_copy(p).wait()
-
-    quarter = u_s.shape[0] // 4
-
-    def u_copy(i):
-        return pltpu.make_async_copy(
-            u_s.at[pl.ds(i * quarter, quarter), :], u_outs[i], u_sem.at[i]
-        )
-
-    for i in range(4):
-        part = pl.ds(i * quarter, quarter)
-        u_s[part, :] = lax.dot_general(
-            lanes(w_s, 0, tiles, part), lanes(f_s, 0, n_c), (((1,), (1,)), ((), ())),
-            preferred_element_type=F32,
-        ).astype(BF)
-        u_copy(i).start()
+        for i in range(4):
+            far_copy(p, i).wait()
+    u_parts(w_s, f_s, 0, mu, outs[1:5])
+    u_parts(w_s, f_s, 2 * mu, mu, outs[5:8])
     for q in range(tiles):
         w_copy(q).wait()
-    for i in range(4):
-        u_copy(i).wait()
 
 
 def weigh(tab, acc, tiles, blocks, pieces, mu, first):
     n_d, n_c = len(blocks), len(pieces)
     panel = blocks[0].shape[0]
-    part = jax.ShapeDtypeStruct((panel // 4, 2 * mu), BF)
+    half = panel // 2
     return pl.pallas_call(
         functools.partial(weigh_kernel, n_d, n_c, mu, first),
-        out_shape=(jax.ShapeDtypeStruct((n_c // 2, panel, 256), BF), part, part, part, part),
+        out_shape=(jax.ShapeDtypeStruct((n_c // 2, panel, 256), BF),)
+        + u_shapes(half, mu, 2) + u_shapes(half, mu, 1),
         in_specs=[SMEM] + [ANY] * (n_d + n_c + 2),
-        out_specs=(ANY,) * 5,
+        out_specs=(ANY,) + (VM,) * 7,
         scratch_shapes=[
             pltpu.VMEM((n_d, panel, mu), BF),
             pltpu.VMEM((n_c, n_d * mu, 128), BF),
-            pltpu.VMEM((n_c, 2 * mu, 128), BF),
+            pltpu.VMEM((n_c, 4 * mu, 128), BF),
             pltpu.VMEM((n_c, panel, 128), BF),
             pltpu.VMEM((n_c // 2, panel, 256), BF),
-            pltpu.VMEM((panel, 2 * mu), BF),
             pltpu.SemaphoreType.DMA((n_d,)),
             pltpu.SemaphoreType.DMA((n_c, n_d)),
-            pltpu.SemaphoreType.DMA((n_c,)),
+            pltpu.SemaphoreType.DMA((n_c, 4)),
             pltpu.SemaphoreType.DMA((n_c,)),
             pltpu.SemaphoreType.DMA((n_c // 2,)),
             pltpu.SemaphoreType.DMA((n_c // 2,)),
-            pltpu.SemaphoreType.DMA((4,)),
         ],
-        compiler_params=pltpu.CompilerParams(vmem_limit_bytes=VMEM_LIMIT),
+        compiler_params=pltpu.CompilerParams(vmem_limit_bytes=52 << 20),
         cost_estimate=pl.CostEstimate(
-            flops=2 * panel * n_c * 128 * (n_d + 2) * mu, bytes_accessed=24 << 20, transcendentals=0
+            flops=2 * panel * n_c * 128 * (n_d + 4) * mu, bytes_accessed=24 << 20, transcendentals=0
         ),
         name="weigh",
     )(tab, acc, tiles, *blocks, *pieces)
 
 
-def spread_kernel(n_c, mu, at, n_out, tab, *refs):
+def spread_kernel(n_c, mu, at, tab, *refs):
     w_ref, c_refs = refs[0], refs[1 : 1 + n_c]
-    o_ref = refs[1 + n_c]
-    w_s, c_s, u_s, w_sem, c_sem, o_sem = refs[2 + n_c :]
-    width = 2 * mu
-
-    def c_copy(ref, p, i, rows):
+    outs, (w_s, c_s, w_sem, c_sem) = refs[1 + n_c : -4], refs[-4:]
+
+    def c_copy(p, j):
+        place = tab[(AT_OWN, AT_OTHER)[j] + at]
         return pltpu.make_async_copy(
-            ref.at[pl.ds(rows, width), :], c_s.at[i, p], c_sem.at[i, p]
+            c_refs[p].at[pl.ds(pl.multiple_of(place * mu, mu), mu), :],
+            c_s.at[p, pl.ds(j * mu, mu), :], c_sem.at[p, j],
         )
 
     w_copy = pltpu.make_async_copy(w_ref, w_s, w_sem)
     w_copy.start()
-    for i in range(n_out):
-        for p in range(n_c):
-            c_copy(c_refs[p], p, i, pl.multiple_of(tab[at + i] * width, width)).start()
-        if i == 0:
-            w_copy.wait()
-
-    def block(i, carry):
-        for p in range(n_c):
-            c_copy(c_refs[0], p, i, 0).wait()
-        u_s[i] = lax.dot_general(
-            lanes(w_s, 0, n_c // 2), lanes(c_s.at[i], 0, n_c), (((1,), (1,)), ((), ())),
-            preferred_element_type=F32,
-        ).astype(BF)
-        pltpu.make_async_copy(u_s.at[i], o_ref.at[i], o_sem.at[i]).start()
-        return carry
-
-    lax.fori_loop(0, n_out, block, 0)
-    for i in range(n_out):
-        pltpu.make_async_copy(u_s.at[i], o_ref.at[i], o_sem.at[i]).wait()
-
-
-def spread(tab, weighted, pieces, mu, at, n_out):
+    for p in range(n_c):
+        for j in range(2):
+            c_copy(p, j).start()
+    w_copy.wait()
+    for p in range(n_c):
+        for j in range(2):
+            c_copy(p, j).wait()
+    u_parts(w_s, c_s, 0, mu, outs)
+
+
+def spread(tab, weighted, pieces, mu, at):
     n_c = len(pieces)
-    panel = weighted.shape[1]
-    width = 2 * mu
+    half = weighted.shape[1] // 2
     return pl.pallas_call(
-        functools.partial(spread_kernel, n_c, mu, at, n_out),
-        out_shape=jax.ShapeDtypeStruct((n_out, panel, width), BF),
-        in_specs=[SMEM] + [ANY] * (1 + n_c),
-        out_specs=ANY,
+        functools.partial(spread_kernel, n_c, mu, at),
+        out_shape=u_shapes(half, mu, 1),
+        in_specs=[SMEM] + [ANY] * (n_c + 1),
+        out_specs=(VM,) * 3,
         scratch_shapes=[
             pltpu.VMEM(weighted.shape, BF),
-            pltpu.VMEM((n_out, n_c, width, 128), BF),
-            pltpu.VMEM((n_out, panel, width), BF),
+            pltpu.VMEM((n_c, 2 * mu, 128), BF),
             pltpu.SemaphoreType.DMA,
-            pltpu.SemaphoreType.DMA((n_out, n_c)),
-            pltpu.SemaphoreType.DMA((n_out,)),
+            pltpu.SemaphoreType.DMA((n_c, 2)),
         ],
-        compiler_params=pltpu.CompilerParams(vmem_limit_bytes=VMEM_LIMIT),
+        compiler_params=pltpu.CompilerParams(vmem_limit_bytes=52 << 20),
         cost_estimate=pl.CostEstimate(
-            flops=2 * panel * n_c * 128 * n_out * width, bytes_accessed=20 << 20, transcendentals=0
+            flops=4 * half * n_c * 128 * mu * 2, bytes_accessed=20 << 20, transcendentals=0
         ),
     )(tab, weighted, *pieces)
 
 
-VM = pl.BlockSpec(memory_space=pltpu.VMEM)
-
-
-def merge_kernel(i, half, first, base_ref, got_ref, out_ref, buf, sem):
-    rows, quarter = buf.shape[0], got_ref.shape[0]
-    copy = pltpu.make_async_copy(base_ref.at[i, pl.ds(half * rows, rows), :], buf, sem)
-    copy.start()
-    copy.wait()
-    with_got = slice(0, quarter) if first else slice(quarter, 2 * quarter)
-    without = slice(quarter, 2 * quarter) if first else slice(0, quarter)
-    out_ref[without, :] = buf[without, :]
-    out_ref[with_got, :] = (buf[with_got, :].astype(F32) + got_ref[...].astype(F32)).astype(BF)
-
-
-def merge(base, got, i, half, first):
-    rows, width = base.shape[1] // 2, base.shape[2]
+def small(kernel, out_shape, operands):
+    many = isinstance(out_shape, tuple)
     return pl.pallas_call(
-        functools.partial(merge_kernel, i, half, first),
-        in_specs=[ANY, VM],
-        out_specs=VM,
-        out_shape=jax.ShapeDtypeStruct((rows, width), BF),
-        scratch_shapes=[pltpu.VMEM((rows, width), BF), pltpu.SemaphoreType.DMA],
-        compiler_params=pltpu.CompilerParams(vmem_limit_bytes=8 << 20),
-        cost_estimate=pl.CostEstimate(
-            flops=rows * width * 64, bytes_accessed=rows * width * 4, transcendentals=0
-        ),
-    )(base, got)
-
-
-def total_kernel(half, mu, tab, base_ref, below_ref, above_ref, sent_ref, kept_ref):
-    rows = sent_ref.shape[0]
-    part = slice(half * rows, (half + 1) * rows)
-    for i, out in ((0, sent_ref), (1, kept_ref)):
-        cols = pl.ds(pl.multiple_of(tab[AT_X + i] * mu, mu), mu)
+        kernel,
+        in_specs=[VM] * len(operands),
+        out_specs=(VM,) * len(out_shape) if many else VM,
+        out_shape=out_shape,
+        compiler_params=pltpu.CompilerParams(vmem_limit_bytes=12 << 20),
+        cost_estimate=pl.CostEstimate(flops=1 << 26, bytes_accessed=4 << 20, transcendentals=0),
+    )(*operands)
+
+
+def pair_kernel(own_ref, got_ref, up_ref, down_ref):
+    rows = up_ref.shape[0]
+    for out, part in ((up_ref, slice(0, rows)), (down_ref, slice(rows, 2 * rows))):
+        out[...] = (own_ref[part, :].astype(F32) + got_ref[part, :].astype(F32)).astype(BF)
+
+
+def merge_a_kernel(i, base_ref, got_ref, out_ref):
+    rows = got_ref.shape[0]
+    there, rest = slice(i * rows, (i + 1) * rows), slice((1 - i) * rows, (2 - i) * rows)
+    out_ref[rest, :] = base_ref[rest, :]
+    out_ref[there, :] = (base_ref[there, :].astype(F32) + got_ref[...].astype(F32)).astype(BF)
+
+
+def merge_b_kernel(i, base_ref, x_ref, got_ref, out_ref):
+    rows = got_ref.shape[0]
+    there, rest = slice(i * rows, (i + 1) * rows), slice((1 - i) * rows, (2 - i) * rows)
+    out_ref[rest, :] = (base_ref[rest, :].astype(F32) + x_ref[rest, :].astype(F32)).astype(BF)
+    out_ref[there, :] = (
+        base_ref[there, :].astype(F32)
+        + x_ref[there, :].astype(F32)
+        + got_ref[...].astype(F32)
+    ).astype(BF)
+
+
+def total_a_kernel(base_ref, below_ref, above_ref, sent_ref, kept_ref):
+    mu = sent_ref.shape[1]
+    for out, cols in ((kept_ref, slice(0, mu)), (sent_ref, slice(mu, 2 * mu))):
         out[...] = (
-            base_ref[0, part, cols].astype(F32)
+            base_ref[:, cols].astype(F32)
             + below_ref[:, cols].astype(F32)
             + above_ref[:, cols].astype(F32)
         ).astype(out.dtype)
 
 
-def totals(tab, base, below, above, half, mu):
-    rows, width = below.shape
-    return pl.pallas_call(
-        functools.partial(total_kernel, half, mu),
-        in_specs=[SMEM, VM, VM, VM],
-        out_specs=(VM, VM),
-        out_shape=(
-            jax.ShapeDtypeStruct((rows, mu), BF),
-            jax.ShapeDtypeStruct((rows, mu), F32),
-        ),
-        compiler_params=pltpu.CompilerParams(vmem_limit_bytes=8 << 20),
-        cost_estimate=pl.CostEstimate(
-            flops=rows * width * 64, bytes_accessed=rows * width * 8, transcendentals=0
-        ),
-    )(tab, base, below, above)
+def total_b_kernel(base_ref, x_ref, below_ref, above_ref, out_ref):
+    out_ref[...] = (
+        base_ref[...].astype(F32)
+        + x_ref[...].astype(F32)
+        + below_ref[...].astype(F32)
+        + above_ref[...].astype(F32)
+    ).astype(BF)
 
 
 def pick_kernel(tab, c_ref, keep_ref, send_ref, buf, in_sem, out_sem):
@@ -426,8 +413,8 @@
 def first_kernel(own_ref, par_ref, r_ref, rp_ref, o_ref):
     depth = r_ref.shape[0]
     o_ref[...] = jnp.dot(
-        own_ref[:, :depth], r_ref[...], preferred_element_type=F32
-    ) + jnp.dot(par_ref[:, :depth], rp_ref[...], preferred_element_type=F32)
+        own_ref[:, depth:], r_ref[...], preferred_element_type=F32
+    ) + jnp.dot(par_ref[:, depth:], rp_ref[...], preferred_element_type=F32)
 
 
 def last_kernel(own_ref, par_ref, r_ref, rp_ref, acc_ref, *outs):
@@ -436,8 +423,8 @@
         part = slice(j * rows, (j + 1) * rows)
         out[...] = (
             acc_ref[part, :]
-            + jnp.dot(own_ref[part, depth:], r_ref[...], preferred_element_type=F32)
-            + jnp.dot(par_ref[part, depth:], rp_ref[...], preferred_element_type=F32)
+            + jnp.dot(own_ref[part, :depth], r_ref[...], preferred_element_type=F32)
+            + jnp.dot(par_ref[part, :depth], rp_ref[...], preferred_element_type=F32)
         ).astype(out.dtype)
 
 
@@ -467,6 +454,7 @@
     core, y, xlo = gx & 1, (gx >> 1) & 3, gx >> 3
     z, xhi = gy >> 1, gy & 1
     sign = 1 - 2 * core
+    panel = collocation.shape[1]
     mu = density.shape[0]
 
     own_piece = lax.dynamic_slice_in_dim(collocation, gy * w, w, 1)
@@ -522,34 +510,53 @@
     hops = [(dx, dy) for dx in (0, 1) for dy in range(4)]
     chips = [((xlo ^ dx) * 4 + ((y + dy) & 3)) * 2 for dx, dy in hops]
     tab = jnp.stack(
-        m_tab + k_tab + [(z + 2) & 3, (z + 1) & 3, (z + 3) & 3, z]
-        + [c + 1 - core for c in chips] + [c + core for c in chips] + [1 - xhi, xhi]
+        m_tab + k_tab
+        + [((z + dz) & 3) * 2 + h for h in (xhi, 1 - xhi) for dz in (2, 1, 3, 0)]
+        + [c + 1 - core for c in chips] + [c + core for c in chips]
     ).astype(jnp.int32)
     blocks = [blocks[j] for j in (0, 1, 2, 3, 4, 5, 7, 6)]
     acc = early(tab, blocks[:6], pieces, mu)
-    weighted, a1, a2, b1, b2 = weigh(tab, acc, tiles, blocks[6:], pieces, mu, 6)
+    weighted, a1, a2, two_b, x2, one_a, one_b, x1 = weigh(
+        tab, acc, tiles, blocks[6:], pieces, mu, 6
+    )
+    half = panel // 2
+    shape = functools.partial(jax.ShapeDtypeStruct, dtype=BF)
 
     a1 = gy_perm(a1, ZUP)
     a2 = gy_perm(a2, ZDOWN)
+    x2 = gy_perm(x2, XHI)
+    x1 = gy_perm(x1, XHI)
+    three_a, three_b, x3 = spread(tab, weighted, pieces, mu, 2)
+    x3 = gy_perm(x3, XHI)
+    zero_a, zero_b, x0 = spread(tab, weighted, pieces, mu, 3)
+    x0 = gy_perm(x0, XHI)
+    b1, b2 = small(pair_kernel, (shape((half // 2, mu)),) * 2, (two_b, x2))
     b1 = gy_perm(b1, ZUP)
     b2 = gy_perm(b2, ZDOWN)
-    near_u = spread(tab, weighted, pieces, mu, AT_Z, 2)
-    zero = spread(tab, weighted, pieces, mu, AT_Z + 2, 1)
-    up_a = gy_perm(merge(near_u, a1, 0, 0, True), ZUP)
-    down_a = gy_perm(merge(near_u, a2, 1, 0, False), ZDOWN)
-    up_b = gy_perm(merge(near_u, b1, 0, 1, True), ZUP)
-    down_b = gy_perm(merge(near_u, b2, 1, 1, False), ZDOWN)
+
+    def merge_a(i, base, got):
+        return small(functools.partial(merge_a_kernel, i), shape((half, 2 * mu)), (base, got))
+
+    def merge_b(i, *operands):
+        return small(functools.partial(merge_b_kernel, i), shape((half, mu)), operands)
+
+    up_a = gy_perm(merge_a(0, one_a, a1), ZUP)
+    down_a = gy_perm(merge_a(1, three_a, a2), ZDOWN)
+    up_b = gy_perm(merge_b(0, one_b, x1, b1), ZUP)
+    down_b = gy_perm(merge_b(1, three_b, x3, b2), ZDOWN)
 
     c_own, c_send = pick(tab, after(collocation, far))
     c_par = gx_perm(c_send, CORE)
 
-    def finish(half, below, above):
-        sent, kept = totals(tab, zero, below, above, half, mu)
-        red = (kept + gy_perm(sent, XHI).astype(F32)).astype(BF)
-        return red, gx_perm(red, CORE)
-
-    part = k_rows(c_own, c_par, *finish(0, up_a, down_a))
-    rows = k_rows(c_own, c_par, *finish(1, up_b, down_b), part)
+    sent, kept = small(
+        total_a_kernel, (shape((half, mu)), jax.ShapeDtypeStruct((half, mu), F32)),
+        (zero_a, up_a, down_a),
+    )
+    got_x = gy_perm(sent, XHI)
+    red_b = small(total_b_kernel, shape((half, mu)), (zero_b, x0, up_b, down_b))
+    part = k_rows(c_own, c_par, red_b, gx_perm(red_b, CORE))
+    red_a = (kept + got_x.astype(F32)).astype(BF)
+    rows = k_rows(c_own, c_par, red_a, gx_perm(red_a, CORE), part)
     total = rows[0]
     for i in (6, 5, 7, 2, 1, 3, 4):
         dx, dy = hops[i]

time: 244 us -> 241 us (0.988)
  Pallas kernels: 70.7 us -> 60.5 us
  waiting for transfers between devices: 68.6 us -> 73.9 us
  starting transfers between devices: 82.3 us -> 86.1 us
    pallas_call x8 -> x9, Pallas kernels: 31.4 us -> 16.3 us  [the longest x2 15.2 us: spread(): pl.pallas_call(functools.partial(spread_kernel, n_c, mu, at), out_shape=u...]
    ppermute x11 -> x14, waiting for transfers between devices: 29.9 us -> 35.3 us  [gy_perm(): return lax.ppermute(x, 'gy', pairs)]
    pallas_call x1, Pallas kernels: 13.9 us -> 18.9 us  [weigh(): pl.pallas_call(functools.partial(weigh_kernel, n_d, n_c, mu, first), out_...]
    unnamed x42 -> x40, local copies, waits for them, and re-layouts: 7.79 us -> 6.15 us
    ppermute x11 -> x14, starting transfers between devices: 18.5 us -> 19.9 us  [gy_perm(): return lax.ppermute(x, 'gy', pairs)]
  transfers between devices with their start and end apart: 46 -> 49, of which waited for: 16 -> 17; matrix products, arithmetic and copies ran while one was open for 3% -> 3% of each run, Pallas kernels for 28% -> 24%
where the time goes in v2:
time: 241 us
  starting transfers between devices  86.1 us (36%)
  waiting for transfers between devices  73.9 us (31%)
  Pallas kernels  60.5 us (25%)
  local copies, waits for them, and re-layouts  13.3 us (6%)
  matrix products  5.69 us (2%)
    ppermute x29, starting transfers between devices, gx_perm(): return lax.ppermute(x, 'gx', pairs)  50 us
    ppermute x14, waiting for transfers between devices, gy_perm(): return lax.ppermute(x, 'gy', pairs)  35.3 us
    ppermute x29, waiting for transfers between devices, gx_perm(): return lax.ppermute(x, 'gx', pairs)  28.3 us
    ppermute x14, starting transfers between devices, gy_perm(): return lax.ppermute(x, 'gy', pairs)  19.9 us
    pallas_call x1, Pallas kernels, weigh(): pl.pallas_call(functools.partial(weigh_kernel, n_d, n_c, mu, first), out_...  18.9 us
    pallas_call x1, Pallas kernels, early(): pl.pallas_call(functools.partial(early_kernel, n_d, n_c, mu), out_shape=j...  16.5 us
    ppermute x6, starting transfers between devices, both_perm(): return lax.ppermute(x, ('gx', 'gy'), pairs)  16.2 us
    pallas_call x2, Pallas kernels, spread(): pl.pallas_call(functools.partial(spread_kernel, n_c, mu, at), out_shape=u...  15.2 us
  transfers between devices with their start and end apart: 49, of which 17 were waited for; matrix products, arithmetic and copies ran while one was open for 3% of the time, Pallas kernels for 24%

profile of v2, /device:TPU:1, one launch (start us, length us, event | category | flops | bytes accessed | tf_op | source)
XLA Modules:
  0.0 240.9 jit_solution(7420343760685024097)
XLA Ops:
  1.7 5.7 %convolution_convert_fusion.refs_0_ = bf16[1024,384]{1,0:T(8,128)(2,1)S(1)} fusion(bf16[3072,1024]{1,0:T(8,128)(2,1)} %c_ref, bf16[384,3072]{1,0:T(8,128)(2,1)S(1)} %copy-done), kind=kOutput, calls=%fused_computation.1 | convolution fusion | flops 2416312320 | bytes 9437184 | tf_op jit(solution)/shard_map/dot_general | solution.py:461
  7.4 3.7 %collective-permute-start.8 = (bf16[1024,384]{1,0:T(8,128)(2,1)S(1)}, bf16[1024,384]{1,0:T(8,128)(2,1)}, u32[]{:S(2)}, u32[]{:S(2)}) collective-permute-start(bf16[1024,384]{1,0:T(8,128)(2,1)S(1)} %convolution_convert_fusion.refs_0_), channel_id=1, source_target_pairs={{0,1},{1,0},{2,3},{3,2},{4,5},{5,4},{6,7},{7,6},{8,9},{9,8},{10,11... | collective-permute-start | bytes 2359304 | tf_op jit(solution)/shard_map/ppermute | solution.py:62
  12.0 3.8 %collective-permute-start.3 = (bf16[1024,384]{1,0:T(8,128)(2,1)S(1)}, bf16[1024,384]{1,0:T(8,128)(2,1)}, u32[]{:S(2)}, u32[]{:S(2)}) collective-permute-start(bf16[1024,384]{1,0:T(8,128)(2,1)S(1)} %convolution_convert_fusion.refs_0_), channel_id=1, source_target_pairs={{0,2},{1,3},{2,4},{3,5},{4,6},{5,7},{6,0},{7,1},{8,14},{9,15},{10,... | collective-permute-start | bytes 2359304 | tf_op jit(solution)/shard_map/ppermute | solution.py:66
  17.3 10.7 %collective-permute-done.8.refs_4_ = bf16[1024,384]{1,0:T(8,128)(2,1)} collective-permute-done((bf16[1024,384]{1,0:T(8,128)(2,1)S(1)}, bf16[1024,384]{1,0:T(8,128)(2,1)}, u32[]{:S(2)}, u32[]{:S(2)}) %collective-permute-start.8) | collective-permute-done | bytes 786464 | tf_op jit(solution)/shard_map/ppermute | solution.py:62
  32.6 3.8 %collective-permute-start.9 = (bf16[1024,384]{1,0:T(8,128)(2,1)}, bf16[1024,384]{1,0:T(8,128)(2,1)S(1)}, u32[]{:S(2)}, u32[]{:S(2)}) collective-permute-start(bf16[1024,384]{1,0:T(8,128)(2,1)} %collective-permute-done.8.refs_4_), channel_id=1, source_target_pairs={{0,2},{1,3},{2,4},{3,5},{4,6},{5,7},{6,0},{7,1},{8,14},{9,15},{10,... | collective-permute-start | bytes 2359304 | tf_op jit(solution)/shard_map/ppermute | solution.py:66
  36.3 8.8 %collective-permute-done.15.refs_14_.refs_12_.refs_9_ = bf16[3072,128]{1,0:T(8,128)(2,1)S(1)} collective-permute-done((bf16[3072,128]{1,0:T(8,128)(2,1)S(1)}, bf16[3072,128]{1,0:T(8,128)(2,1)S(1)}, u32[]{:S(2)}, u32[]{:S(2)}) %collective-permute-start.15) | collective-permute-done | bytes 786464 | tf_op jit(solution)/shard_map/ppermute | solution.py:58
  45.1 3.8 %collective-permute-start.5 = (bf16[1024,384]{1,0:T(8,128)(2,1)}, bf16[1024,384]{1,0:T(8,128)(2,1)S(1)}, u32[]{:S(2)}, u32[]{:S(2)}) collective-permute-start(bf16[1024,384]{1,0:T(8,128)(2,1)} %collective-permute-done.4), channel_id=1, source_target_pairs={{0,2},{1,3},{2,4},{3,5},{4,6},{5,7},{6,0},{7,1},{8,14},{9,15},{10,... | collective-permute-start | bytes 2359304 | tf_op jit(solution)/shard_map/ppermute | solution.py:66
  53.5 4.7 %collective-permute-done.5 = bf16[1024,384]{1,0:T(8,128)(2,1)S(1)} collective-permute-done((bf16[1024,384]{1,0:T(8,128)(2,1)}, bf16[1024,384]{1,0:T(8,128)(2,1)S(1)}, u32[]{:S(2)}, u32[]{:S(2)}) %collective-permute-start.5) | collective-permute-done | bytes 786464 | tf_op jit(solution)/shard_map/ppermute | solution.py:66
  60.9 5.7 %collective-permute-done.7.refs_3_ = bf16[1024,384]{1,0:T(8,128)(2,1)S(1)} collective-permute-done((bf16[1024,384]{1,0:T(8,128)(2,1)}, bf16[1024,384]{1,0:T(8,128)(2,1)S(1)}, u32[]{:S(2)}, u32[]{:S(2)}) %collective-permute-start.7) | collective-permute-done | bytes 786464 | tf_op jit(solution)/shard_map/ppermute | solution.py:66
  73.9 4.3 %collective-permute-done.1.refs_12_.refs_10_.refs_7_ = bf16[3072,128]{1,0:T(8,128)(2,1)} collective-permute-done((bf16[3072,128]{1,0:T(8,128)(2,1)S(1)}, bf16[3072,128]{1,0:T(8,128)(2,1)}, u32[]{:S(2)}, u32[]{:S(2)}) %collective-permute-start.1) | collective-permute-done | bytes 786464 | tf_op jit(solution)/shard_map/ppermute | solution.py:58
  78.2 4.4 %collective-permute-start.20 = (bf16[3072,128]{1,0:T(8,128)(2,1)S(1)}, bf16[3072,128]{1,0:T(8,128)(2,1)}, u32[]{:S(2)}, u32[]{:S(2)}) collective-permute-start(bf16[3072,128]{1,0:T(8,128)(2,1)S(1)} %collective-permute-done.17.refs_16_.refs_14_.refs_11_), channel_id=1, source_target_pairs={{0,8},{8,0},{16,24},{24,16},{32,40},{40,32},{48,56},{56,48},{64,72... | collective-permute-start | bytes 2359304 | tf_op jit(solution)/shard_map/ppermute | solution.py:58
  86.7 4.4 %collective-permute-start.22 = (bf16[3072,128]{1,0:T(8,128)(2,1)}, bf16[3072,128]{1,0:T(8,128)(2,1)}, u32[]{:S(2)}, u32[]{:S(2)}) collective-permute-start(bf16[3072,128]{1,0:T(8,128)(2,1)} %collective-permute-done.21.refs_20_.refs_18_.refs_15_), channel_id=1, source_target_pairs={{0,8},{8,0},{16,24},{24,16},{32,40},{40,32},{48,56},{56,48},{64,72... | collective-permute-start | bytes 2359304 | tf_op jit(solution)/shard_map/ppermute | solution.py:58
  91.1 4.0 %collective-permute-done.18.refs_17_.refs_15_.refs_12_ = bf16[3072,128]{1,0:T(8,128)(2,1)} collective-permute-done((bf16[3072,128]{1,0:T(8,128)(2,1)S(1)}, bf16[3072,128]{1,0:T(8,128)(2,1)}, u32[]{:S(2)}, u32[]{:S(2)}) %collective-permute-start.18) | collective-permute-done | bytes 786464 | tf_op jit(solution)/shard_map/ppermute | solution.py:58
  95.1 4.5 %collective-permute-start.19 = (bf16[3072,128]{1,0:T(8,128)(2,1)}, bf16[3072,128]{1,0:T(8,128)(2,1)}, u32[]{:S(2)}, u32[]{:S(2)}) collective-permute-start(bf16[3072,128]{1,0:T(8,128)(2,1)} %collective-permute-done.18.refs_17_.refs_15_.refs_12_), channel_id=1, source_target_pairs={{0,8},{8,0},{16,24},{24,16},{32,40},{40,32},{48,56},{56,48},{64,72... | collective-permute-start | bytes 2359304 | tf_op jit(solution)/shard_map/ppermute | solution.py:58
  100.3 5.3 %copy.6 = bf16[1024,16,1,128]{3,0,1,2:T(8,128)(2,1)} copy(bf16[1024,16,1,128]{3,1,2,0:T(8,128)(2,1)} %param.5) | data formatting | bytes 8388608 | tf_op jit(solution)/shard_map/optimization_barrier | solution.py:70
  105.6 5.3 %pick.1 = (bf16[1536,1024]{1,0:T(8,128)(2,1)}, bf16[1536,1024]{1,0:T(8,128)(2,1)}) custom-call(s32[48]{0:T(128)} %stack.177.tab, bf16[3072,1024]{1,0:T(8,128)(2,1)} %c_ref), custom_call_target="tpu_custom_call" | custom-call | flops 1073741824 | bytes 12582912 | tf_op jit(solution)/shard_map/pick/pallas_call | solution.py:396
  112.8 16.5 %early.1.refs_0_ = bf16[8,1024,256]{2,1,0:T(8,128)(2,1)} custom-call(s32[48]{0:T(128)} %stack.177.tab, bf16[1024,384]{1,0:T(8,128)(2,1)} %copy-done.14, bf16[1024,384]{1,0:T(8,128)(2,1)} %collective-permute-done.3.refs_1_, bf16[1024,384]{1,0:T(8,128)(2,1)} %copy-done.18, bf16[1024,384]{1,0:T(8,128)(2,1)} %copy-done.16, ...), custom_call_target="tpu_custom_call" | custom-call | flops 9663676416 | bytes 25165824 | tf_op jit(solution)/shard_map/early/pallas_call | solution.py:128
  130.3 18.9 %weigh.1 = (bf16[8,1024,256]{2,1,0:T(8,128)(2,1)}, bf16[256,768]{1,0:T(8,128)(2,1)S(1)}, bf16[256,768]{1,0:T(8,128)(2,1)S(1)}, bf16[512,384]{1,0:T(8,128)(2,1)S(...) custom-call(s32[48]{0:T(128)S(1)} %copy-done.6, ...), custom_call_target="tpu_custom_call" | custom-call | flops 9663676416 | bytes 25165824 | tf_op jit(solution)/shard_map/weigh/pallas_call | solution.py:247
  154.9 7.6 %shard_map.39 = (bf16[512,768]{1,0:T(8,128)(2,1)S(1)}, bf16[512,384]{1,0:T(8,128)(2,1)S(1)}, bf16[512,384]{1,0:T(8,128)(2,1)S(1)}) custom-call(s32[48]{0:T(128)S(1)} %copy-done.6, bf16[8,1024,256]{2,1,0:T(8,128)(2,1)} %get-tuple-element.39.refs_0_, bf16[3072,128]{1,0:T(8,128)(2,1)} %copy-done.7, bf16[3072,128]{1,0:T(8,128)(2,1)} %copy-done.9, ...), custom_call_target="tpu_custom_call" | custom-call | flops 3221225472 | bytes 20971520 | tf_op jit(solution)/shard_map/pallas_call | solution.py:300
  165.6 6.1 %collective-permute-done.35.got_ref = bf16[512,384]{1,0:T(8,128)(2,1)S(1)} collective-permute-done((bf16[512,384]{1,0:T(8,128)(2,1)S(1)}, bf16[512,384]{1,0:T(8,128)(2,1)S(1)}, u32[]{:S(2)}, u32[]{:S(2)}) %collective-permute-start.35) | collective-permute-done | bytes 393248 | tf_op jit(solution)/shard_map/ppermute | solution.py:62
  173.7 11.9 %collective-permute-done.36.got_ref = bf16[256,384]{1,0:T(8,128)(2,1)S(1)} collective-permute-done((bf16[256,384]{1,0:T(8,128)(2,1)S(1)}, bf16[256,384]{1,0:T(8,128)(2,1)S(1)}, u32[]{:S(2)}, u32[]{:S(2)}) %collective-permute-start.36) | collective-permute-done | bytes 196640 | tf_op jit(solution)/shard_map/ppermute | solution.py:62
  185.6 7.6 %shard_map.37 = (bf16[512,768]{1,0:T(8,128)(2,1)S(1)}, bf16[512,384]{1,0:T(8,128)(2,1)S(1)}, bf16[512,384]{1,0:T(8,128)(2,1)S(1)}) custom-call(s32[48]{0:T(128)S(1)} %copy-done.6, bf16[8,1024,256]{2,1,0:T(8,128)(2,1)} %get-tuple-element.39.refs_0_, bf16[3072,128]{1,0:T(8,128)(2,1)} %copy-done.7, bf16[3072,128]{1,0:T(8,128)(2,1)} %copy-done.9, ...), custom_call_target="tpu_custom_call" | custom-call | flops 3221225472 | bytes 20971520 | tf_op jit(solution)/shard_map/pallas_call | solution.py:300
  199.7 3.5 %collective-permute-done.33.x_ref = bf16[512,384]{1,0:T(8,128)(2,1)S(1)} collective-permute-done((bf16[512,384]{1,0:T(8,128)(2,1)S(1)}, bf16[512,384]{1,0:T(8,128)(2,1)S(1)}, u32[]{:S(2)}, u32[]{:S(2)}) %collective-permute-start.33) | collective-permute-done | bytes 393248 | tf_op jit(solution)/shard_map/ppermute | solution.py:62
  204.6 5.1 %collective-permute-start.41 = (bf16[512,384]{1,0:T(8,128)(2,1)S(1)}, bf16[512,384]{1,0:T(8,128)(2,1)S(1)}, u32[]{:S(2)}, u32[]{:S(2)}) collective-permute-start(bf16[512,384]{1,0:T(8,128)(2,1)S(1)} %shard_map.45.r_ref), channel_id=1, source_target_pairs={{0,8},{8,0},{16,24},{24,16},{32,40},{40,32},{48,56},{56,48},{64,72... | collective-permute-start | bytes 1179656 | tf_op jit(solution)/shard_map/ppermute | solution.py:58
  (134 shorter events, 80.6 us)
Async XLA Ops:
  7.4 20.6 %collective-permute-start.8 = (bf16[1024,384]{1,0:T(8,128)(2,1)S(1)}, bf16[1024,384]{1,0:T(8,128)(2,1)}, u32[]{:S(2)}, u32[]{:S(2)}) collective-permute-start(bf16[1024,384]{1,0:T(8,128)(2,1)S(1)} %convolution_convert_fusion.refs_0_), channel_id=1, source_target_pairs={{0,1},{1,0},{2,3},{3,2},{4,5},{5,4},{6,7},{7,6},{8,9},{9,8},{10,11... | collective-permute-start | bytes 2359304 | tf_op jit(solution)/shard_map/ppermute | solution.py:62
  11.0 20.0 %collective-permute-start.4 = (bf16[1024,384]{1,0:T(8,128)(2,1)S(1)}, bf16[1024,384]{1,0:T(8,128)(2,1)}, u32[]{:S(2)}, u32[]{:S(2)}) collective-permute-start(bf16[1024,384]{1,0:T(8,128)(2,1)S(1)} %convolution_convert_fusion.refs_0_), channel_id=1, source_target_pairs={{0,8},{8,0},{16,24},{24,16},{32,40},{40,32},{48,56},{56,48},{64,72... | collective-permute-start | bytes 2359304 | tf_op jit(solution)/shard_map/ppermute | solution.py:58
  12.0 20.6 %collective-permute-start.3 = (bf16[1024,384]{1,0:T(8,128)(2,1)S(1)}, bf16[1024,384]{1,0:T(8,128)(2,1)}, u32[]{:S(2)}, u32[]{:S(2)}) collective-permute-start(bf16[1024,384]{1,0:T(8,128)(2,1)S(1)} %convolution_convert_fusion.refs_0_), channel_id=1, source_target_pairs={{0,2},{1,3},{2,4},{3,5},{4,6},{5,7},{6,0},{7,1},{8,14},{9,15},{10,... | collective-permute-start | bytes 2359304 | tf_op jit(solution)/shard_map/ppermute | solution.py:66
  16.9 28.2 %collective-permute-start.15 = (bf16[3072,128]{1,0:T(8,128)(2,1)S(1)}, bf16[3072,128]{1,0:T(8,128)(2,1)S(1)}, u32[]{:S(2)}, u32[]{:S(2)}) collective-permute-start(bf16[3072,128]{1,0:T(8,128)(2,1)S(1)} %constant_dynamic-slice_fusion.refs_6_.refs_4_.refs_1_), channel_id=1, source_target_pairs={{0,64},{8,72},{16,80},{24,88},{32,96},{40,104},{48,112},{56,120},{... | collective-permute-start | bytes 2359304 | tf_op jit(solution)/shard_map/ppermute | solution.py:58
  17.3 31.6 %collective-permute-start.10 = (bf16[3072,128]{1,0:T(8,128)(2,1)S(1)}, bf16[3072,128]{1,0:T(8,128)(2,1)S(1)}, u32[]{:S(2)}, u32[]{:S(2)}) collective-permute-start(bf16[3072,128]{1,0:T(8,128)(2,1)S(1)} %constant_dynamic-slice_fusion.refs_6_.refs_4_.refs_1_), channel_id=1, source_target_pairs={{0,8},{8,0},{16,24},{24,16},{32,40},{40,32},{48,56},{56,48},{64,72... | collective-permute-start | bytes 2359304 | tf_op jit(solution)/shard_map/ppermute | solution.py:58
  28.0 21.0 %collective-permute-start = (bf16[3072,128]{1,0:T(8,128)(2,1)S(1)}, bf16[3072,128]{1,0:T(8,128)(2,1)S(1)}, u32[]{:S(2)}, u32[]{:S(2)}) collective-permute-start(bf16[3072,128]{1,0:T(8,128)(2,1)S(1)} %constant_dynamic-slice_fusion.refs_6_.refs_4_.refs_1_), channel_id=1, source_target_pairs={{0,16},{8,56},{16,32},{24,8},{32,48},{40,24},{48,0},{56,40},{64,80... | collective-permute-start | bytes 2359304 | tf_op jit(solution)/shard_map/ppermute | solution.py:58
  31.1 20.7 %collective-permute-start.24 = (bf16[1024,384]{1,0:T(8,128)(2,1)}, bf16[1024,384]{1,0:T(8,128)(2,1)S(1)}, u32[]{:S(2)}, u32[]{:S(2)}) collective-permute-start(bf16[1024,384]{1,0:T(8,128)(2,1)} %collective-permute-done.8.refs_4_), channel_id=1, source_target_pairs={{0,8},{8,0},{16,24},{24,16},{32,40},{40,32},{48,56},{56,48},{64,72... | collective-permute-start | bytes 2359304 | tf_op jit(solution)/shard_map/ppermute | solution.py:58
  32.6 19.6 %collective-permute-start.9 = (bf16[1024,384]{1,0:T(8,128)(2,1)}, bf16[1024,384]{1,0:T(8,128)(2,1)S(1)}, u32[]{:S(2)}, u32[]{:S(2)}) collective-permute-start(bf16[1024,384]{1,0:T(8,128)(2,1)} %collective-permute-done.8.refs_4_), channel_id=1, source_target_pairs={{0,2},{1,3},{2,4},{3,5},{4,6},{5,7},{6,0},{7,1},{8,14},{9,15},{10,... | collective-permute-start | bytes 2359304 | tf_op jit(solution)/shard_map/ppermute | solution.py:66
  49.0 20.3 %collective-permute-start.17 = (bf16[3072,128]{1,0:T(8,128)(2,1)S(1)}, bf16[3072,128]{1,0:T(8,128)(2,1)S(1)}, u32[]{:S(2)}, u32[]{:S(2)}) collective-permute-start(bf16[3072,128]{1,0:T(8,128)(2,1)S(1)} %collective-permute-done.15.refs_14_.refs_12_.refs_9_), channel_id=1, source_target_pairs={{0,16},{8,56},{16,32},{24,8},{32,48},{40,24},{48,0},{56,40},{64,80... | collective-permute-start | bytes 2359304 | tf_op jit(solution)/shard_map/ppermute | solution.py:58
  51.8 20.5 %collective-permute-start.16 = (bf16[3072,128]{1,0:T(8,128)(2,1)S(1)}, bf16[3072,128]{1,0:T(8,128)(2,1)S(1)}, u32[]{:S(2)}, u32[]{:S(2)}) collective-permute-start(bf16[3072,128]{1,0:T(8,128)(2,1)S(1)} %collective-permute-done.15.refs_14_.refs_12_.refs_9_), channel_id=1, source_target_pairs={{0,8},{8,0},{16,24},{24,16},{32,40},{40,32},{48,56},{56,48},{64,72... | collective-permute-start | bytes 2359304 | tf_op jit(solution)/shard_map/ppermute | solution.py:58
  52.1 20.3 %collective-permute-start.11 = (bf16[3072,128]{1,0:T(8,128)(2,1)S(1)}, bf16[3072,128]{1,0:T(8,128)(2,1)}, u32[]{:S(2)}, u32[]{:S(2)}) collective-permute-start(bf16[3072,128]{1,0:T(8,128)(2,1)S(1)} %collective-permute-done.10.refs_7_.refs_5_.refs_2_), channel_id=1, source_target_pairs={{0,16},{8,56},{16,32},{24,8},{32,48},{40,24},{48,0},{56,40},{64,80... | collective-permute-start | bytes 2359304 | tf_op jit(solution)/shard_map/ppermute | solution.py:58
  73.0 22.1 %collective-permute-start.18 = (bf16[3072,128]{1,0:T(8,128)(2,1)S(1)}, bf16[3072,128]{1,0:T(8,128)(2,1)}, u32[]{:S(2)}, u32[]{:S(2)}) collective-permute-start(bf16[3072,128]{1,0:T(8,128)(2,1)S(1)} %collective-permute-done.16.refs_15_.refs_13_.refs_10_), channel_id=1, source_target_pairs={{0,16},{8,56},{16,32},{24,8},{32,48},{40,24},{48,0},{56,40},{64,80... | collective-permute-start | bytes 2359304 | tf_op jit(solution)/shard_map/ppermute | solution.py:58
  78.2 32.6 %collective-permute-start.20 = (bf16[3072,128]{1,0:T(8,128)(2,1)S(1)}, bf16[3072,128]{1,0:T(8,128)(2,1)}, u32[]{:S(2)}, u32[]{:S(2)}) collective-permute-start(bf16[3072,128]{1,0:T(8,128)(2,1)S(1)} %collective-permute-done.17.refs_16_.refs_14_.refs_11_), channel_id=1, source_target_pairs={{0,8},{8,0},{16,24},{24,16},{32,40},{40,32},{48,56},{56,48},{64,72... | collective-permute-start | bytes 2359304 | tf_op jit(solution)/shard_map/ppermute | solution.py:58
  82.6 28.4 %collective-permute-start.12 = (bf16[3072,128]{1,0:T(8,128)(2,1)}, bf16[3072,128]{1,0:T(8,128)(2,1)}, u32[]{:S(2)}, u32[]{:S(2)}) collective-permute-start(bf16[3072,128]{1,0:T(8,128)(2,1)} %collective-permute-done.11.refs_9_.refs_7_.refs_4_), channel_id=1, source_target_pairs={{0,8},{8,0},{16,24},{24,16},{32,40},{40,32},{48,56},{56,48},{64,72... | collective-permute-start | bytes 2359304 | tf_op jit(solution)/shard_map/ppermute | solution.py:58
  84.1 28.7 %collective-permute-start.14 = (bf16[3072,128]{1,0:T(8,128)(2,1)}, bf16[3072,128]{1,0:T(8,128)(2,1)}, u32[]{:S(2)}, u32[]{:S(2)}) collective-permute-start(bf16[3072,128]{1,0:T(8,128)(2,1)} %collective-permute-done.1.refs_12_.refs_10_.refs_7_), channel_id=1, source_target_pairs={{0,8},{8,0},{16,24},{24,16},{32,40},{40,32},{48,56},{56,48},{64,72... | collective-permute-start | bytes 2359304 | tf_op jit(solution)/shard_map/ppermute | solution.py:58
  86.7 26.2 %collective-permute-start.22 = (bf16[3072,128]{1,0:T(8,128)(2,1)}, bf16[3072,128]{1,0:T(8,128)(2,1)}, u32[]{:S(2)}, u32[]{:S(2)}) collective-permute-start(bf16[3072,128]{1,0:T(8,128)(2,1)} %collective-permute-done.21.refs_20_.refs_18_.refs_15_), channel_id=1, source_target_pairs={{0,8},{8,0},{16,24},{24,16},{32,40},{40,32},{48,56},{56,48},{64,72... | collective-permute-start | bytes 2359304 | tf_op jit(solution)/shard_map/ppermute | solution.py:58
  95.1 17.7 %collective-permute-start.19 = (bf16[3072,128]{1,0:T(8,128)(2,1)}, bf16[3072,128]{1,0:T(8,128)(2,1)}, u32[]{:S(2)}, u32[]{:S(2)}) collective-permute-start(bf16[3072,128]{1,0:T(8,128)(2,1)} %collective-permute-done.18.refs_17_.refs_15_.refs_12_), channel_id=1, source_target_pairs={{0,8},{8,0},{16,24},{24,16},{32,40},{40,32},{48,56},{56,48},{64,72... | collective-permute-start | bytes 2359304 | tf_op jit(solution)/shard_map/ppermute | solution.py:58
  110.9 104.2 %collective-permute-start.2 = (bf16[1536,1024]{1,0:T(8,128)(2,1)}, bf16[1536,1024]{1,0:T(8,128)(2,1)S(1)}, u32[]{:S(2)}, u32[]{:S(2)}) collective-permute-start(bf16[1536,1024]{1,0:T(8,128)(2,1)} %get-tuple-element.37), channel_id=1, source_target_pairs={{0,8},{8,0},{16,24},{24,16},{32,40},{40,32},{48,56},{56,48},{64,72... | collective-permute-start | bytes 9437192 | tf_op jit(solution)/shard_map/ppermute | solution.py:58
  111.1 18.3 %collective-permute-start.23 = (bf16[1024,384]{1,0:T(8,128)(2,1)}, bf16[1024,384]{1,0:T(8,128)(2,1)S(1)}, u32[]{:S(2)}, u32[]{:S(2)}) collective-permute-start(bf16[1024,384]{1,0:T(8,128)(2,1)} %copy-done.15), channel_id=1, source_target_pairs={{0,2},{1,3},{2,4},{3,5},{4,6},{5,7},{6,0},{7,1},{8,14},{9,15},{10,... | collective-permute-start | bytes 2359304 | tf_op jit(solution)/shard_map/ppermute | solution.py:66
  151.9 20.0 %collective-permute-start.34 = (bf16[512,384]{1,0:T(8,128)(2,1)}, bf16[512,384]{1,0:T(8,128)(2,1)S(1)}, u32[]{:S(2)}, u32[]{:S(2)}) collective-permute-start(bf16[512,384]{1,0:T(8,128)(2,1)} %get-tuple-element.50), channel_id=1, source_target_pairs={{0,1},{1,0},{2,3},{3,2},{4,5},{5,4},{6,7},{7,6},{8,9},{9,8},{10,11... | collective-permute-start | bytes 1179656 | tf_op jit(solution)/shard_map/ppermute | solution.py:62
  153.6 18.0 %collective-permute-start.35 = (bf16[512,384]{1,0:T(8,128)(2,1)S(1)}, bf16[512,384]{1,0:T(8,128)(2,1)S(1)}, u32[]{:S(2)}, u32[]{:S(2)}) collective-permute-start(bf16[512,384]{1,0:T(8,128)(2,1)S(1)} %get-tuple-element.52), channel_id=1, source_target_pairs={{0,1},{1,0},{2,3},{3,2},{4,5},{5,4},{6,7},{7,6},{8,9},{9,8},{10,11... | collective-permute-start | bytes 1179656 | tf_op jit(solution)/shard_map/ppermute | solution.py:62
  162.6 34.2 %collective-permute-start.28 = (bf16[512,768]{1,0:T(8,128)(2,1)S(1)}, bf16[512,768]{1,0:T(8,128)(2,1)S(1)}, u32[]{:S(2)}, u32[]{:S(2)}) collective-permute-start(bf16[512,768]{1,0:T(8,128)(2,1)S(1)} %shard_map.38), channel_id=1, source_target_pairs={{0,2},{1,3},{2,4},{3,5},{4,6},{5,7},{6,0},{7,1},{8,10},{9,11},{10,... | collective-permute-start | bytes 2359304 | tf_op jit(solution)/shard_map/ppermute | solution.py:62
  162.9 35.3 %collective-permute-start.30 = (bf16[512,768]{1,0:T(8,128)(2,1)S(1)}, bf16[512,768]{1,0:T(8,128)(2,1)S(1)}, u32[]{:S(2)}, u32[]{:S(2)}) collective-permute-start(bf16[512,768]{1,0:T(8,128)(2,1)S(1)} %shard_map.40), channel_id=1, source_target_pairs={{0,6},{1,7},{2,0},{3,1},{4,2},{5,3},{6,4},{7,5},{8,14},{9,15},{10,... | collective-permute-start | bytes 2359304 | tf_op jit(solution)/shard_map/ppermute | solution.py:62
  171.9 21.5 %collective-permute-start.38 = (bf16[512,384]{1,0:T(8,128)(2,1)S(1)}, bf16[512,384]{1,0:T(8,128)(2,1)S(1)}, u32[]{:S(2)}, u32[]{:S(2)}) collective-permute-start(bf16[512,384]{1,0:T(8,128)(2,1)S(1)} %get-tuple-element.55), channel_id=1, source_target_pairs={{0,1},{1,0},{2,3},{3,2},{4,5},{5,4},{6,7},{7,6},{8,9},{9,8},{10,11... | collective-permute-start | bytes 1179656 | tf_op jit(solution)/shard_map/ppermute | solution.py:62
  (45 other events, 749.7 us)

commit v3 on v2

--- a/solution.py
+++ b/solution.py
@@ -49,6 +49,7 @@
 XLO = gx_pairs(lambda a, b, c: (1 - a, b, c))
 YSPLIT = gx_pairs(lambda a, b, c: (a, b + 1 if c == 0 else b - 1, c))
 ZSPLIT = both_pairs(lambda c, z, h: (z + 1 if c == 0 else z - 1, h))
+ZBACK = both_pairs(lambda c, z, h: (z - 1 if c == 0 else z + 1, h))
 XHI = gy_pairs(lambda z, h: (z, 1 - h))
 ZUP = gy_pairs(lambda z, h: (z + 1, h))
 ZDOWN = gy_pairs(lambda z, h: (z - 1, h))
@@ -467,8 +468,7 @@
     piece_x = gx_perm(own_piece, XLO)
     near_other = gx_perm(other, YSPLIT)
     d_near = both_perm(own_t, ZSPLIT)
-    d_other = gx_perm(own_t, CORE)
-    d_near_other = both_perm(d_other, ZSPLIT)
+    d_back = both_perm(own_t, ZBACK)
     far = gx_perm(near, YSPLIT)
     own_x = gy_perm(own_t, XHI)
     d_far = both_perm(d_near, ZSPLIT)
@@ -477,9 +477,8 @@
     near_x = gx_perm(px, YSPLIT)
     near_other_x = gx_perm(other_x, YSPLIT)
     dx = own_x
-    d_other_x = gx_perm(dx, CORE)
     d_near_x = both_perm(dx, ZSPLIT)
-    d_near_other_x = both_perm(d_other_x, ZSPLIT)
+    d_back_x = both_perm(dx, ZBACK)
     far_x = gx_perm(near_x, YSPLIT)
     d_far_x = both_perm(d_near_x, ZSPLIT)
     pieces = [
@@ -491,8 +490,8 @@
         far_x, gx_perm(far_x, CORE),
     ]
     blocks = [
-        own_t, d_near, gx_perm(d_near_other, CORE), d_far,
-        own_x, d_near_x, gx_perm(d_near_other_x, CORE), d_far_x,
+        own_t, d_near, d_back, d_far,
+        own_x, d_near_x, d_back_x, d_far_x,
     ]
     k_tab = []
     for xl in (xlo, 1 - xlo):

time: 241 us -> 238 us (0.988)
  starting transfers between devices: 86.1 us -> 77.6 us
  waiting for transfers between devices: 73.9 us -> 80.3 us
    ppermute x29 -> x25, waiting for transfers between devices: 28.3 us -> 44.1 us  [gx_perm(): return lax.ppermute(x, 'gx', pairs)]
    ppermute x6, waiting for transfers between devices: 10.3 us -> 3.62 us  [both_perm(): return lax.ppermute(x, ('gx', 'gy'), pairs)]
    ppermute x6, starting transfers between devices: 16.2 us -> 9.48 us  [both_perm(): return lax.ppermute(x, ('gx', 'gy'), pairs)]
    ppermute x14, waiting for transfers between devices: 35.3 us -> 32.5 us  [gy_perm(): return lax.ppermute(x, 'gy', pairs)]
    ppermute x29 -> x25, starting transfers between devices: 50 us -> 47.4 us  [gx_perm(): return lax.ppermute(x, 'gx', pairs)]
    unnamed x40 -> x38, local copies, waits for them, and re-layouts: 6.15 us -> 5.25 us
  transfers between devices with their start and end apart: 49 -> 45, of which waited for: 17 -> 20; matrix products, arithmetic and copies ran while one was open for 3% -> 3% of each run, Pallas kernels for 24% -> 25%
where the time goes in v3:
time: 238 us
  waiting for transfers between devices  80.3 us (34%)
  starting transfers between devices  77.6 us (33%)
  Pallas kernels  60.5 us (25%)
  local copies, waits for them, and re-layouts  12.4 us (5%)
  matrix products  5.69 us (2%)
    ppermute x25, starting transfers between devices, gx_perm(): return lax.ppermute(x, 'gx', pairs)  47.4 us
    ppermute x25, waiting for transfers between devices, gx_perm(): return lax.ppermute(x, 'gx', pairs)  44.1 us
    ppermute x14, waiting for transfers between devices, gy_perm(): return lax.ppermute(x, 'gy', pairs)  32.5 us
    ppermute x14, starting transfers between devices, gy_perm(): return lax.ppermute(x, 'gy', pairs)  20.7 us
    pallas_call x1, Pallas kernels, weigh(): pl.pallas_call(functools.partial(weigh_kernel, n_d, n_c, mu, first), out_...  18.8 us
    pallas_call x1, Pallas kernels, early(): pl.pallas_call(functools.partial(early_kernel, n_d, n_c, mu), out_shape=j...  16.5 us
    pallas_call x2, Pallas kernels, spread(): pl.pallas_call(functools.partial(spread_kernel, n_c, mu, at), out_shape=u...  15.2 us
    ppermute x6, starting transfers between devices, both_perm(): return lax.ppermute(x, ('gx', 'gy'), pairs)  9.48 us
  transfers between devices with their start and end apart: 45, of which 20 were waited for; matrix products, arithmetic and copies ran while one was open for 3% of the time, Pallas kernels for 25%

profile of v3, /device:TPU:1, one launch (start us, length us, event | category | flops | bytes accessed | tf_op | source)
XLA Modules:
  0.0 237.6 jit_solution(4125576515026561304)
XLA Ops:
  1.7 5.7 %convolution_convert_fusion.refs_0_ = bf16[1024,384]{1,0:T(8,128)(2,1)S(1)} fusion(bf16[3072,1024]{1,0:T(8,128)(2,1)} %c_ref, bf16[384,3072]{1,0:T(8,128)(2,1)S(1)} %copy-done), kind=kOutput, calls=%fused_computation.1 | convolution fusion | flops 2416312320 | bytes 9437184 | tf_op jit(solution)/shard_map/dot_general | solution.py:462
  7.4 3.7 %collective-permute-start.6 = (bf16[1024,384]{1,0:T(8,128)(2,1)S(1)}, bf16[1024,384]{1,0:T(8,128)(2,1)}, u32[]{:S(2)}, u32[]{:S(2)}) collective-permute-start(bf16[1024,384]{1,0:T(8,128)(2,1)S(1)} %convolution_convert_fusion.refs_0_), channel_id=1, source_target_pairs={{0,1},{1,0},{2,3},{3,2},{4,5},{5,4},{6,7},{7,6},{8,9},{9,8},{10,11... | collective-permute-start | bytes 2359304 | tf_op jit(solution)/shard_map/ppermute | solution.py:63
  17.9 10.1 %collective-permute-done.6.refs_4_ = bf16[1024,384]{1,0:T(8,128)(2,1)} collective-permute-done((bf16[1024,384]{1,0:T(8,128)(2,1)S(1)}, bf16[1024,384]{1,0:T(8,128)(2,1)}, u32[]{:S(2)}, u32[]{:S(2)}) %collective-permute-start.6) | collective-permute-done | bytes 786464 | tf_op jit(solution)/shard_map/ppermute | solution.py:63
  31.1 3.8 %collective-permute-start.7 = (bf16[1024,384]{1,0:T(8,128)(2,1)}, bf16[1024,384]{1,0:T(8,128)(2,1)}, u32[]{:S(2)}, u32[]{:S(2)}) collective-permute-start(bf16[1024,384]{1,0:T(8,128)(2,1)} %collective-permute-done.6.refs_4_), channel_id=1, source_target_pairs={{0,2},{1,3},{2,4},{3,5},{4,6},{5,7},{6,0},{7,1},{8,14},{9,15},{10,... | collective-permute-start | bytes 2359304 | tf_op jit(solution)/shard_map/ppermute | solution.py:67
  35.0 10.3 %collective-permute-done.13.refs_14_.refs_12_.refs_9_ = bf16[3072,128]{1,0:T(8,128)(2,1)S(1)} collective-permute-done((bf16[3072,128]{1,0:T(8,128)(2,1)S(1)}, bf16[3072,128]{1,0:T(8,128)(2,1)S(1)}, u32[]{:S(2)}, u32[]{:S(2)}) %collective-permute-start.13) | collective-permute-done | bytes 786464 | tf_op jit(solution)/shard_map/ppermute | solution.py:59
  53.1 3.9 %collective-permute-done.15.refs_16_.refs_14_.refs_11_ = bf16[3072,128]{1,0:T(8,128)(2,1)S(1)} collective-permute-done((bf16[3072,128]{1,0:T(8,128)(2,1)S(1)}, bf16[3072,128]{1,0:T(8,128)(2,1)S(1)}, u32[]{:S(2)}, u32[]{:S(2)}) %collective-permute-start.15) | collective-permute-done | bytes 786464 | tf_op jit(solution)/shard_map/ppermute | solution.py:59
  56.9 3.1 %collective-permute-start.19 = (bf16[3072,128]{1,0:T(8,128)(2,1)S(1)}, bf16[3072,128]{1,0:T(8,128)(2,1)}, u32[]{:S(2)}, u32[]{:S(2)}) collective-permute-start(bf16[3072,128]{1,0:T(8,128)(2,1)S(1)} %collective-permute-done.15.refs_16_.refs_14_.refs_11_), channel_id=1, source_target_pairs={{0,16},{8,56},{16,32},{24,8},{32,48},{40,24},{48,0},{56,40},{64,80... | collective-permute-start | bytes 2359304 | tf_op jit(solution)/shard_map/ppermute | solution.py:59
  60.1 5.2 %collective-permute-done.9.refs_9_.refs_7_.refs_4_ = bf16[3072,128]{1,0:T(8,128)(2,1)S(1)} collective-permute-done((bf16[3072,128]{1,0:T(8,128)(2,1)S(1)}, bf16[3072,128]{1,0:T(8,128)(2,1)S(1)}, u32[]{:S(2)}, u32[]{:S(2)}) %collective-permute-start.9) | collective-permute-done | bytes 786464 | tf_op jit(solution)/shard_map/ppermute | solution.py:59
  68.4 5.4 %collective-permute-done.1.refs_12_.refs_10_.refs_7_ = bf16[3072,128]{1,0:T(8,128)(2,1)} collective-permute-done((bf16[3072,128]{1,0:T(8,128)(2,1)S(1)}, bf16[3072,128]{1,0:T(8,128)(2,1)}, u32[]{:S(2)}, u32[]{:S(2)}) %collective-permute-start.1) | collective-permute-done | bytes 786464 | tf_op jit(solution)/shard_map/ppermute | solution.py:59
  76.8 5.4 %collective-permute-done.19.refs_20_.refs_18_.refs_15_ = bf16[3072,128]{1,0:T(8,128)(2,1)} collective-permute-done((bf16[3072,128]{1,0:T(8,128)(2,1)S(1)}, bf16[3072,128]{1,0:T(8,128)(2,1)}, u32[]{:S(2)}, u32[]{:S(2)}) %collective-permute-start.19) | collective-permute-done | bytes 786464 | tf_op jit(solution)/shard_map/ppermute | solution.py:59
  85.3 5.4 %collective-permute-done.16.refs_17_.refs_15_.refs_12_ = bf16[3072,128]{1,0:T(8,128)(2,1)} collective-permute-done((bf16[3072,128]{1,0:T(8,128)(2,1)S(1)}, bf16[3072,128]{1,0:T(8,128)(2,1)}, u32[]{:S(2)}, u32[]{:S(2)}) %collective-permute-start.16) | collective-permute-done | bytes 786464 | tf_op jit(solution)/shard_map/ppermute | solution.py:59
  90.6 3.1 %collective-permute-start.17 = (bf16[3072,128]{1,0:T(8,128)(2,1)}, bf16[3072,128]{1,0:T(8,128)(2,1)}, u32[]{:S(2)}, u32[]{:S(2)}) collective-permute-start(bf16[3072,128]{1,0:T(8,128)(2,1)} %collective-permute-done.16.refs_17_.refs_15_.refs_12_), channel_id=1, source_target_pairs={{0,8},{8,0},{16,24},{24,16},{32,40},{40,32},{48,56},{56,48},{64,72... | collective-permute-start | bytes 2359304 | tf_op jit(solution)/shard_map/ppermute | solution.py:59
  94.4 5.3 %copy.6 = bf16[1024,16,1,128]{3,0,1,2:T(8,128)(2,1)} copy(bf16[1024,16,1,128]{3,1,2,0:T(8,128)(2,1)} %param.5) | data formatting | bytes 8388608 | tf_op jit(solution)/shard_map/optimization_barrier | solution.py:71
  99.7 5.3 %pick.1 = (bf16[1536,1024]{1,0:T(8,128)(2,1)}, bf16[1536,1024]{1,0:T(8,128)(2,1)}) custom-call(s32[48]{0:T(128)} %stack.177.tab, bf16[3072,1024]{1,0:T(8,128)(2,1)} %c_ref), custom_call_target="tpu_custom_call" | custom-call | flops 1073741824 | bytes 12582912 | tf_op jit(solution)/shard_map/pick/pallas_call | solution.py:397
  109.3 16.5 %early.1.refs_0_ = bf16[8,1024,256]{2,1,0:T(8,128)(2,1)} custom-call(s32[48]{0:T(128)} %stack.177.tab, bf16[1024,384]{1,0:T(8,128)(2,1)} %copy-done.15, bf16[1024,384]{1,0:T(8,128)(2,1)} %collective-permute-done.3.refs_1_, bf16[1024,384]{1,0:T(8,128)(2,1)} %copy-done.16, bf16[1024,384]{1,0:T(8,128)(2,1)} %copy-done.17, ...), custom_call_target="tpu_custom_call" | custom-call | flops 9663676416 | bytes 25165824 | tf_op jit(solution)/shard_map/early/pallas_call | solution.py:129
  126.9 18.8 %weigh.1 = (bf16[8,1024,256]{2,1,0:T(8,128)(2,1)}, bf16[256,768]{1,0:T(8,128)(2,1)S(1)}, bf16[256,768]{1,0:T(8,128)(2,1)S(1)}, bf16[512,384]{1,0:T(8,128)(2,1)S(...) custom-call(s32[48]{0:T(128)S(1)} %copy-done.6, ...), custom_call_target="tpu_custom_call" | custom-call | flops 9663676416 | bytes 25165824 | tf_op jit(solution)/shard_map/weigh/pallas_call | solution.py:248
  152.2 7.6 %shard_map.39 = (bf16[512,768]{1,0:T(8,128)(2,1)S(1)}, bf16[512,384]{1,0:T(8,128)(2,1)S(1)}, bf16[512,384]{1,0:T(8,128)(2,1)S(1)}) custom-call(s32[48]{0:T(128)S(1)} %copy-done.6, bf16[8,1024,256]{2,1,0:T(8,128)(2,1)} %get-tuple-element.39.refs_0_, bf16[3072,128]{1,0:T(8,128)(2,1)} %copy-done.7, bf16[3072,128]{1,0:T(8,128)(2,1)} %copy-done.9, ...), custom_call_target="tpu_custom_call" | custom-call | flops 3221225472 | bytes 20971520 | tf_op jit(solution)/shard_map/pallas_call | solution.py:301
  162.9 5.5 %collective-permute-done.31.got_ref = bf16[512,384]{1,0:T(8,128)(2,1)S(1)} collective-permute-done((bf16[512,384]{1,0:T(8,128)(2,1)S(1)}, bf16[512,384]{1,0:T(8,128)(2,1)S(1)}, u32[]{:S(2)}, u32[]{:S(2)}) %collective-permute-start.31) | collective-permute-done | bytes 393248 | tf_op jit(solution)/shard_map/ppermute | solution.py:63
  170.5 11.9 %collective-permute-done.32.got_ref = bf16[256,384]{1,0:T(8,128)(2,1)S(1)} collective-permute-done((bf16[256,384]{1,0:T(8,128)(2,1)S(1)}, bf16[256,384]{1,0:T(8,128)(2,1)S(1)}, u32[]{:S(2)}, u32[]{:S(2)}) %collective-permute-start.32) | collective-permute-done | bytes 196640 | tf_op jit(solution)/shard_map/ppermute | solution.py:63
  182.4 7.6 %shard_map.37 = (bf16[512,768]{1,0:T(8,128)(2,1)S(1)}, bf16[512,384]{1,0:T(8,128)(2,1)S(1)}, bf16[512,384]{1,0:T(8,128)(2,1)S(1)}) custom-call(s32[48]{0:T(128)S(1)} %copy-done.6, bf16[8,1024,256]{2,1,0:T(8,128)(2,1)} %get-tuple-element.39.refs_0_, bf16[3072,128]{1,0:T(8,128)(2,1)} %copy-done.7, bf16[3072,128]{1,0:T(8,128)(2,1)} %copy-done.9, ...), custom_call_target="tpu_custom_call" | custom-call | flops 3221225472 | bytes 20971520 | tf_op jit(solution)/shard_map/pallas_call | solution.py:301
  200.8 6.2 %collective-permute-start.37 = (bf16[512,384]{1,0:T(8,128)(2,1)S(1)}, bf16[512,384]{1,0:T(8,128)(2,1)S(1)}, u32[]{:S(2)}, u32[]{:S(2)}) collective-permute-start(bf16[512,384]{1,0:T(8,128)(2,1)S(1)} %shard_map.45.r_ref), channel_id=1, source_target_pairs={{0,8},{8,0},{16,24},{24,16},{32,40},{40,32},{48,56},{56,48},{64,72... | collective-permute-start | bytes 1179656 | tf_op jit(solution)/shard_map/ppermute | solution.py:59
  208.0 3.9 %collective-permute-start.28 = (bf16[512,384]{1,0:T(8,128)(2,1)S(1)}, bf16[512,384]{1,0:T(8,128)(2,1)S(1)}, u32[]{:S(2)}, u32[]{:S(2)}) collective-permute-start(bf16[512,384]{1,0:T(8,128)(2,1)S(1)} %add_convert_fusion.r_ref), channel_id=1, source_target_pairs={{0,8},{8,0},{16,24},{24,16},{32,40},{40,32},{48,56},{56,48},{64,72... | collective-permute-start | bytes 1179656 | tf_op jit(solution)/shard_map/ppermute | solution.py:59
  222.1 3.1 %collective-permute-start.40 = (bf16[192,384]{1,0:T(8,128)(2,1)S(1)}, bf16[192,384]{1,0:T(8,128)(2,1)S(1)}, u32[]{:S(2)}, u32[]{:S(2)}) collective-permute-start(bf16[192,384]{1,0:T(8,128)(2,1)S(1)} %get-tuple-element.60), channel_id=1, source_target_pairs={{0,112},{8,120},{16,64},{24,72},{32,80},{40,88},{48,96},{56,104},{... | collective-permute-start | bytes 442376 | tf_op jit(solution)/shard_map/ppermute | solution.py:59
  233.4 3.4 %collective-permute-done.42 = bf16[192,384]{1,0:T(8,128)(2,1)S(1)} collective-permute-done((bf16[192,384]{1,0:T(8,128)(2,1)S(1)}, bf16[192,384]{1,0:T(8,128)(2,1)S(1)}, u32[]{:S(2)}, u32[]{:S(2)}) %collective-permute-start.42) | collective-permute-done | bytes 147488 | tf_op jit(solution)/shard_map/ppermute | solution.py:59
  (124 shorter events, 77.3 us)
Async XLA Ops:
  7.4 20.6 %collective-permute-start.6 = (bf16[1024,384]{1,0:T(8,128)(2,1)S(1)}, bf16[1024,384]{1,0:T(8,128)(2,1)}, u32[]{:S(2)}, u32[]{:S(2)}) collective-permute-start(bf16[1024,384]{1,0:T(8,128)(2,1)S(1)} %convolution_convert_fusion.refs_0_), channel_id=1, source_target_pairs={{0,1},{1,0},{2,3},{3,2},{4,5},{5,4},{6,7},{7,6},{8,9},{9,8},{10,11... | collective-permute-start | bytes 2359304 | tf_op jit(solution)/shard_map/ppermute | solution.py:63
  11.0 20.0 %collective-permute-start.4 = (bf16[1024,384]{1,0:T(8,128)(2,1)S(1)}, bf16[1024,384]{1,0:T(8,128)(2,1)S(1)}, u32[]{:S(2)}, u32[]{:S(2)}) collective-permute-start(bf16[1024,384]{1,0:T(8,128)(2,1)S(1)} %convolution_convert_fusion.refs_0_), channel_id=1, source_target_pairs={{0,6},{1,7},{2,0},{3,1},{4,2},{5,3},{6,4},{7,5},{8,10},{9,11},{10,... | collective-permute-start | bytes 2359304 | tf_op jit(solution)/shard_map/ppermute | solution.py:67
  12.7 22.2 %collective-permute-start.3 = (bf16[1024,384]{1,0:T(8,128)(2,1)S(1)}, bf16[1024,384]{1,0:T(8,128)(2,1)}, u32[]{:S(2)}, u32[]{:S(2)}) collective-permute-start(bf16[1024,384]{1,0:T(8,128)(2,1)S(1)} %convolution_convert_fusion.refs_0_), channel_id=1, source_target_pairs={{0,2},{1,3},{2,4},{3,5},{4,6},{5,7},{6,0},{7,1},{8,14},{9,15},{10,... | collective-permute-start | bytes 2359304 | tf_op jit(solution)/shard_map/ppermute | solution.py:67
  16.0 29.3 %collective-permute-start.13 = (bf16[3072,128]{1,0:T(8,128)(2,1)S(1)}, bf16[3072,128]{1,0:T(8,128)(2,1)S(1)}, u32[]{:S(2)}, u32[]{:S(2)}) collective-permute-start(bf16[3072,128]{1,0:T(8,128)(2,1)S(1)} %constant_dynamic-slice_fusion.refs_6_.refs_4_.refs_1_), channel_id=1, source_target_pairs={{0,64},{8,72},{16,80},{24,88},{32,96},{40,104},{48,112},{56,120},{... | collective-permute-start | bytes 2359304 | tf_op jit(solution)/shard_map/ppermute | solution.py:59
  16.4 31.6 %collective-permute-start.8 = (bf16[3072,128]{1,0:T(8,128)(2,1)S(1)}, bf16[3072,128]{1,0:T(8,128)(2,1)S(1)}, u32[]{:S(2)}, u32[]{:S(2)}) collective-permute-start(bf16[3072,128]{1,0:T(8,128)(2,1)S(1)} %constant_dynamic-slice_fusion.refs_6_.refs_4_.refs_1_), channel_id=1, source_target_pairs={{0,8},{8,0},{16,24},{24,16},{32,40},{40,32},{48,56},{56,48},{64,72... | collective-permute-start | bytes 2359304 | tf_op jit(solution)/shard_map/ppermute | solution.py:59
  28.0 20.3 %collective-permute-start = (bf16[3072,128]{1,0:T(8,128)(2,1)S(1)}, bf16[3072,128]{1,0:T(8,128)(2,1)S(1)}, u32[]{:S(2)}, u32[]{:S(2)}) collective-permute-start(bf16[3072,128]{1,0:T(8,128)(2,1)S(1)} %constant_dynamic-slice_fusion.refs_6_.refs_4_.refs_1_), channel_id=1, source_target_pairs={{0,16},{8,56},{16,32},{24,8},{32,48},{40,24},{48,0},{56,40},{64,80... | collective-permute-start | bytes 2359304 | tf_op jit(solution)/shard_map/ppermute | solution.py:59
  31.1 18.7 %collective-permute-start.7 = (bf16[1024,384]{1,0:T(8,128)(2,1)}, bf16[1024,384]{1,0:T(8,128)(2,1)}, u32[]{:S(2)}, u32[]{:S(2)}) collective-permute-start(bf16[1024,384]{1,0:T(8,128)(2,1)} %collective-permute-done.6.refs_4_), channel_id=1, source_target_pairs={{0,2},{1,3},{2,4},{3,5},{4,6},{5,7},{6,0},{7,1},{8,14},{9,15},{10,... | collective-permute-start | bytes 2359304 | tf_op jit(solution)/shard_map/ppermute | solution.py:67
  34.8 17.7 %collective-permute-start.5 = (bf16[1024,384]{1,0:T(8,128)(2,1)}, bf16[1024,384]{1,0:T(8,128)(2,1)S(1)}, u32[]{:S(2)}, u32[]{:S(2)}) collective-permute-start(bf16[1024,384]{1,0:T(8,128)(2,1)} %collective-permute-done.3.refs_1_), channel_id=1, source_target_pairs={{0,2},{1,3},{2,4},{3,5},{4,6},{5,7},{6,0},{7,1},{8,14},{9,15},{10,... | collective-permute-start | bytes 2359304 | tf_op jit(solution)/shard_map/ppermute | solution.py:67
  49.8 18.5 %collective-permute-start.11 = (bf16[3072,128]{1,0:T(8,128)(2,1)S(1)}, bf16[3072,128]{1,0:T(8,128)(2,1)S(1)}, u32[]{:S(2)}, u32[]{:S(2)}) collective-permute-start(bf16[3072,128]{1,0:T(8,128)(2,1)S(1)} %collective-permute-done.refs_8_.refs_6_.refs_3_), channel_id=1, source_target_pairs={{0,8},{8,0},{16,24},{24,16},{32,40},{40,32},{48,56},{56,48},{64,72... | collective-permute-start | bytes 2359304 | tf_op jit(solution)/shard_map/ppermute | solution.py:59
  52.5 21.3 %collective-permute-start.1 = (bf16[3072,128]{1,0:T(8,128)(2,1)S(1)}, bf16[3072,128]{1,0:T(8,128)(2,1)}, u32[]{:S(2)}, u32[]{:S(2)}) collective-permute-start(bf16[3072,128]{1,0:T(8,128)(2,1)S(1)} %collective-permute-done.refs_8_.refs_6_.refs_3_), channel_id=1, source_target_pairs={{0,16},{8,56},{16,32},{24,8},{32,48},{40,24},{48,0},{56,40},{64,80... | collective-permute-start | bytes 2359304 | tf_op jit(solution)/shard_map/ppermute | solution.py:59
  56.9 25.3 %collective-permute-start.19 = (bf16[3072,128]{1,0:T(8,128)(2,1)S(1)}, bf16[3072,128]{1,0:T(8,128)(2,1)}, u32[]{:S(2)}, u32[]{:S(2)}) collective-permute-start(bf16[3072,128]{1,0:T(8,128)(2,1)S(1)} %collective-permute-done.15.refs_16_.refs_14_.refs_11_), channel_id=1, source_target_pairs={{0,16},{8,56},{16,32},{24,8},{32,48},{40,24},{48,0},{56,40},{64,80... | collective-permute-start | bytes 2359304 | tf_op jit(solution)/shard_map/ppermute | solution.py:59
  60.1 30.6 %collective-permute-start.16 = (bf16[3072,128]{1,0:T(8,128)(2,1)S(1)}, bf16[3072,128]{1,0:T(8,128)(2,1)}, u32[]{:S(2)}, u32[]{:S(2)}) collective-permute-start(bf16[3072,128]{1,0:T(8,128)(2,1)S(1)} %collective-permute-done.14.refs_15_.refs_13_.refs_10_), channel_id=1, source_target_pairs={{0,16},{8,56},{16,32},{24,8},{32,48},{40,24},{48,0},{56,40},{64,80... | collective-permute-start | bytes 2359304 | tf_op jit(solution)/shard_map/ppermute | solution.py:59
  65.4 39.6 %collective-permute-start.18 = (bf16[3072,128]{1,0:T(8,128)(2,1)S(1)}, bf16[3072,128]{1,0:T(8,128)(2,1)}, u32[]{:S(2)}, u32[]{:S(2)}) collective-permute-start(bf16[3072,128]{1,0:T(8,128)(2,1)S(1)} %collective-permute-done.15.refs_16_.refs_14_.refs_11_), channel_id=1, source_target_pairs={{0,8},{8,0},{16,24},{24,16},{32,40},{40,32},{48,56},{56,48},{64,72... | collective-permute-start | bytes 2359304 | tf_op jit(solution)/shard_map/ppermute | solution.py:59
  68.3 38.4 %collective-permute-start.10 = (bf16[3072,128]{1,0:T(8,128)(2,1)S(1)}, bf16[3072,128]{1,0:T(8,128)(2,1)}, u32[]{:S(2)}, u32[]{:S(2)}) collective-permute-start(bf16[3072,128]{1,0:T(8,128)(2,1)S(1)} %collective-permute-done.9.refs_9_.refs_7_.refs_4_), channel_id=1, source_target_pairs={{0,8},{8,0},{16,24},{24,16},{32,40},{40,32},{48,56},{56,48},{64,72... | collective-permute-start | bytes 2359304 | tf_op jit(solution)/shard_map/ppermute | solution.py:59
  73.8 35.4 %collective-permute-start.12 = (bf16[3072,128]{1,0:T(8,128)(2,1)}, bf16[3072,128]{1,0:T(8,128)(2,1)}, u32[]{:S(2)}, u32[]{:S(2)}) collective-permute-start(bf16[3072,128]{1,0:T(8,128)(2,1)} %collective-permute-done.1.refs_12_.refs_10_.refs_7_), channel_id=1, source_target_pairs={{0,8},{8,0},{16,24},{24,16},{32,40},{40,32},{48,56},{56,48},{64,72... | collective-permute-start | bytes 2359304 | tf_op jit(solution)/shard_map/ppermute | solution.py:59
  82.2 27.1 %collective-permute-start.20 = (bf16[3072,128]{1,0:T(8,128)(2,1)}, bf16[3072,128]{1,0:T(8,128)(2,1)}, u32[]{:S(2)}, u32[]{:S(2)}) collective-permute-start(bf16[3072,128]{1,0:T(8,128)(2,1)} %collective-permute-done.19.refs_20_.refs_18_.refs_15_), channel_id=1, source_target_pairs={{0,8},{8,0},{16,24},{24,16},{32,40},{40,32},{48,56},{56,48},{64,72... | collective-permute-start | bytes 2359304 | tf_op jit(solution)/shard_map/ppermute | solution.py:59
  90.6 18.7 %collective-permute-start.17 = (bf16[3072,128]{1,0:T(8,128)(2,1)}, bf16[3072,128]{1,0:T(8,128)(2,1)}, u32[]{:S(2)}, u32[]{:S(2)}) collective-permute-start(bf16[3072,128]{1,0:T(8,128)(2,1)} %collective-permute-done.16.refs_17_.refs_15_.refs_12_), channel_id=1, source_target_pairs={{0,8},{8,0},{16,24},{24,16},{32,40},{40,32},{48,56},{56,48},{64,72... | collective-permute-start | bytes 2359304 | tf_op jit(solution)/shard_map/ppermute | solution.py:59
  105.0 20.8 %collective-permute-start.22 = (bf16[1024,384]{1,0:T(8,128)(2,1)}, bf16[1024,384]{1,0:T(8,128)(2,1)S(1)}, u32[]{:S(2)}, u32[]{:S(2)}) collective-permute-start(bf16[1024,384]{1,0:T(8,128)(2,1)} %collective-permute-done.6.refs_4_), channel_id=1, source_target_pairs={{0,6},{1,7},{2,0},{3,1},{4,2},{5,3},{6,4},{7,5},{8,10},{9,11},{10,... | collective-permute-start | bytes 2359304 | tf_op jit(solution)/shard_map/ppermute | solution.py:67
  106.7 105.2 %collective-permute-start.2 = (bf16[1536,1024]{1,0:T(8,128)(2,1)}, bf16[1536,1024]{1,0:T(8,128)(2,1)S(1)}, u32[]{:S(2)}, u32[]{:S(2)}) collective-permute-start(bf16[1536,1024]{1,0:T(8,128)(2,1)} %get-tuple-element.37), channel_id=1, source_target_pairs={{0,8},{8,0},{16,24},{24,16},{32,40},{40,32},{48,56},{56,48},{64,72... | collective-permute-start | bytes 9437192 | tf_op jit(solution)/shard_map/ppermute | solution.py:59
  109.2 17.7 %collective-permute-start.21 = (bf16[1024,384]{1,0:T(8,128)(2,1)}, bf16[1024,384]{1,0:T(8,128)(2,1)}, u32[]{:S(2)}, u32[]{:S(2)}) collective-permute-start(bf16[1024,384]{1,0:T(8,128)(2,1)} %collective-permute-done.7.refs_5_), channel_id=1, source_target_pairs={{0,2},{1,3},{2,4},{3,5},{4,6},{5,7},{6,0},{7,1},{8,14},{9,15},{10,... | collective-permute-start | bytes 2359304 | tf_op jit(solution)/shard_map/ppermute | solution.py:67
  149.2 19.6 %collective-permute-start.30 = (bf16[512,384]{1,0:T(8,128)(2,1)}, bf16[512,384]{1,0:T(8,128)(2,1)S(1)}, u32[]{:S(2)}, u32[]{:S(2)}) collective-permute-start(bf16[512,384]{1,0:T(8,128)(2,1)} %get-tuple-element.50), channel_id=1, source_target_pairs={{0,1},{1,0},{2,3},{3,2},{4,5},{5,4},{6,7},{7,6},{8,9},{9,8},{10,11... | collective-permute-start | bytes 1179656 | tf_op jit(solution)/shard_map/ppermute | solution.py:63
  160.0 33.6 %collective-permute-start.24 = (bf16[512,768]{1,0:T(8,128)(2,1)S(1)}, bf16[512,768]{1,0:T(8,128)(2,1)S(1)}, u32[]{:S(2)}, u32[]{:S(2)}) collective-permute-start(bf16[512,768]{1,0:T(8,128)(2,1)S(1)} %shard_map.38), channel_id=1, source_target_pairs={{0,2},{1,3},{2,4},{3,5},{4,6},{5,7},{6,0},{7,1},{8,10},{9,11},{10,... | collective-permute-start | bytes 2359304 | tf_op jit(solution)/shard_map/ppermute | solution.py:63
  160.2 34.7 %collective-permute-start.26 = (bf16[512,768]{1,0:T(8,128)(2,1)S(1)}, bf16[512,768]{1,0:T(8,128)(2,1)S(1)}, u32[]{:S(2)}, u32[]{:S(2)}) collective-permute-start(bf16[512,768]{1,0:T(8,128)(2,1)S(1)} %shard_map.40), channel_id=1, source_target_pairs={{0,6},{1,7},{2,0},{3,1},{4,2},{5,3},{6,4},{7,5},{8,14},{9,15},{10,... | collective-permute-start | bytes 2359304 | tf_op jit(solution)/shard_map/ppermute | solution.py:63
  168.8 21.4 %collective-permute-start.34 = (bf16[512,384]{1,0:T(8,128)(2,1)S(1)}, bf16[512,384]{1,0:T(8,128)(2,1)S(1)}, u32[]{:S(2)}, u32[]{:S(2)}) collective-permute-start(bf16[512,384]{1,0:T(8,128)(2,1)S(1)} %get-tuple-element.55), channel_id=1, source_target_pairs={{0,1},{1,0},{2,3},{3,2},{4,5},{5,4},{6,7},{7,6},{8,9},{9,8},{10,11... | collective-permute-start | bytes 1179656 | tf_op jit(solution)/shard_map/ppermute | solution.py:63
  (40 other events, 646.6 us)
